TPU v7x, 32 devices: a whole 2x2x4 slice. The times are simulated.
32 devices in a mesh: px: 8 (over z, y), py: 4 (over x, core).
Axes of the slice: x: 2, y: 2, z: 4, core: 2. Of those that a mesh axis runs over, the one named last changes fastest.
Arguments:
- flow_field: bfloat16 [64, 128, 128, 128], P(None, 'px', 'py'), may hold values from -6 to 6
- cotangent: bfloat16 [64, 128, 128, 128], P(None, 'px', 'py'), may hold values from -6 to 6
- tucker_core: float32 [16, 16, 8, 8, 8], replicated, may hold values from -6 to 6
- in_factor: float32 [64, 16], replicated, may hold values from -0.75 to 0.75
- out_factor: float32 [64, 16], replicated, may hold values from -1.5 to 1.5
- first_factor: float32 [32, 8], replicated, may hold values from -2 to 2
- second_factor: float32 [32, 8], replicated, may hold values from -2 to 2
- third_factor: float32 [32, 8], replicated, may hold values from -2 to 2
Outputs:
- output_field: bfloat16 [64, 128, 128, 128], P(None, 'px', 'py')
- core_grad: float32 [16, 16, 8, 8, 8], replicated
- in_grad: float32 [64, 16], replicated
- out_grad: float32 [64, 16], replicated
- first_grad: float32 [32, 8], replicated
- second_grad: float32 [32, 8], replicated
- third_grad: float32 [32, 8], replicated
All inputs are finite; a program needn't handle non-finite values.
Results may differ from a plain program's by a relative error of at most 0.001.
Values sent between devices are 32-bit elements; how exact they have to be, the bound alone decides.
A program may use at most 192 MiB of HBM per device.

v0:
```python
import functools
import math

import jax
import jax.numpy as jnp
import numpy as np
from jax import lax
from jax.experimental import pallas as pl
from jax.experimental.pallas import tpu as pltpu
from jax.sharding import PartitionSpec as P

NX = 128
NY = 128
NZ = 128
M1 = 32
M2 = 32
M3 = 32


HIGHEST = lax.Precision.HIGHEST


def turn_table(count, length):
    position = jnp.arange(count)
    frequency = jnp.where(position < count // 2, position, position - count)
    cells_at = jnp.arange(length)
    phase = frequency[None, :] * cells_at[:, None] % length
    angle = 2.0 * math.pi / length * phase.astype(jnp.float32)
    cosine = jnp.cos(angle)
    sine = jnp.sin(angle)
    upper = jnp.stack([cosine, -sine], axis=1)
    lower = jnp.stack([sine, cosine], axis=1)
    return jnp.stack([upper, lower])


def depth_table(length, count):
    cells_at = jnp.arange(length)
    frequency = jnp.arange(count)
    phase = cells_at[:, None] * frequency[None, :] % length
    angle = 2.0 * math.pi / length * phase.astype(jnp.float32)
    return jnp.concatenate([jnp.cos(angle), -jnp.sin(angle)], axis=1)


def to_modes(fields, depth_tables):
    across = turn_table(M2, NY)
    along = turn_table(M1, NX)
    spectra = []
    for member, z_table in zip(fields, depth_tables):
        channels, rows_here, cols_here, depth_len = member.shape
        flat = jnp.dot(member.reshape(-1, depth_len), z_table, precision=HIGHEST)
        spectra.append(flat.reshape(channels, rows_here, cols_here, 2, M3))
    members = lax.all_to_all(tuple(spectra), "py", split_axis=4, concat_axis=2, tiled=True)
    lines = tuple(
        (jnp.einsum("cxypm,pyqk->cxqkm", member, across, precision=HIGHEST) for member in members)
    )
    members = (
        lax.all_to_all(lines[0], "px", split_axis=3, concat_axis=1, tiled=True),
        lax.all_to_all(lines[1], "px", split_axis=3, concat_axis=1, tiled=True),
    )
    return tuple(
        (jnp.einsum("cxpkm,pxqj->cqjkm", member, along, precision=HIGHEST) for member in members)
    )


def to_space(modes, depth_weights):
    across = turn_table(M2, NY)
    along = turn_table(M1, NX)
    depth_base = depth_table(NZ, M3).T.reshape(2, M3, NZ)
    lines = tuple(
        (jnp.einsum("cqjkm,pxqj->cpxkm", member, along, precision=HIGHEST) for member in modes)
    )
    members = (
        lax.all_to_all(lines[0], "px", split_axis=2, concat_axis=3, tiled=True),
        lax.all_to_all(lines[1], "px", split_axis=2, concat_axis=3, tiled=True),
    )
    columns = tuple(
        (jnp.einsum("cqxkm,pyqk->cpxym", member, across, precision=HIGHEST) for member in members)
    )
    members = (
        lax.all_to_all(columns[0], "py", split_axis=3, concat_axis=4, tiled=True),
        lax.all_to_all(columns[1], "py", split_axis=3, concat_axis=4, tiled=True),
    )
    return tuple(
        (
            jnp.einsum(
                "cpxyk,pkn->cxyn", member, depth_base * weight_row[None, :, None], precision=HIGHEST
            )
            for member, weight_row in zip(members, depth_weights)
        )
    )


def shards(
    flow_field,
    cotangent,
    tucker_core,
    in_factor,
    out_factor,
    first_factor,
    second_factor,
    third_factor,
):
    inverse_count = 1.0 / (NX * NY * NZ)
    weights = jnp.where(jnp.arange(M3) == 0, 1.0, 2.0).astype(jnp.float32)
    unit_weights = jnp.ones((M3,), jnp.float32)
    base_table = depth_table(NZ, M3)
    weighted_table = base_table * jnp.concatenate([weights, weights])[None, :]
    block_second = M2 // lax.axis_size("px")
    block_third = M3 // lax.axis_size("py")
    start_second = lax.axis_index("px") * block_second
    start_third = lax.axis_index("py") * block_third

    def build_kernel(core_arg, first_arg, second_arg, third_arg):
        second_rows = lax.dynamic_slice_in_dim(second_arg, start_second, block_second, 0)
        third_rows = lax.dynamic_slice_in_dim(third_arg, start_third, block_third, 0)
        partial_core = jnp.einsum("abrst,mt->abrsm", core_arg, third_rows, precision=HIGHEST)
        partial_core = jnp.einsum("abrsm,ks->abrkm", partial_core, second_rows, precision=HIGHEST)
        return jnp.einsum("abrkm,jr->abjkm", partial_core, first_arg, precision=HIGHEST)

    kernel, pullback = jax.vjp(build_kernel, tucker_core, first_factor, second_factor, third_factor)
    field_wide = flow_field.astype(jnp.float32)
    back_wide = cotangent.astype(jnp.float32)
    lifted_grid = jnp.einsum("cxyn,ca->axyn", field_wide, in_factor, precision=HIGHEST)
    back_grid = jnp.einsum("cxyn,cb->bxyn", back_wide, out_factor, precision=HIGHEST)
    lifted, back_mixed = to_modes((lifted_grid, back_grid), (base_table, weighted_table))
    back_mixed = back_mixed * inverse_count
    mixed = jnp.einsum("abjkm,apjkm->bpjkm", kernel, lifted, precision=HIGHEST)
    grad_kernel = jnp.einsum("bpjkm,apjkm->abjkm", back_mixed, lifted, precision=HIGHEST)
    back_lifted = jnp.einsum("abjkm,bpjkm->apjkm", kernel, back_mixed, precision=HIGHEST)
    mixed_grid, lifted_back = to_space((mixed, back_lifted), (weights, unit_weights))
    mixed_grid = mixed_grid * inverse_count
    output_field = jnp.einsum("ob,bxyn->oxyn", out_factor, mixed_grid, precision=HIGHEST).astype(
        jnp.bfloat16
    )
    grad_out = jnp.einsum("oxyn,bxyn->ob", back_wide, mixed_grid, precision=HIGHEST)
    grad_in = jnp.einsum("ixyn,axyn->ia", field_wide, lifted_back, precision=HIGHEST)
    grad_core, grad_first, grad_second, grad_third = pullback(grad_kernel)
    totals = lax.psum(
        (grad_core, grad_in, grad_out, grad_first, grad_second, grad_third), ("px", "py")
    )
    return (output_field, totals[0], totals[1], totals[2], totals[3], totals[4], totals[5])


BF16 = jnp.bfloat16
F32 = jnp.float32
NN = (((1,), (0,)), ((), ()))
NT = (((1,), (1,)), ((), ()))
TN = (((0,), (0,)), ((), ()))
MESH = pl.DeviceIdType.MESH
VMEM_LIMIT = 60 * 1024 * 1024
SUB = 16
LANES = 128


def mul(a, b, dims=NN):
    return lax.dot_general(a, b, dims, preferred_element_type=F32)


def exact(a, b, dims=NN):
    return lax.dot_general(a, b, dims, precision=HIGHEST, preferred_element_type=F32)


def halves(x):
    high = x.astype(BF16)
    return high, (x - high.astype(F32)).astype(BF16)


def mul3(a, b, dims=NN):
    (ah, al), (bh, bl) = a, b
    return mul(ah, bh, dims) + (mul(ah, bl, dims) + mul(al, bh, dims))


def np_halves(x):
    x = np.asarray(x, np.float32)
    high = x.astype(BF16)
    return np.stack([high, (x - high.astype(np.float32)).astype(BF16)])


def np_turn(count, length):
    position = np.arange(count)
    frequency = np.where(position < count // 2, position, position - count)
    phase = frequency[None, :] * np.arange(length)[:, None] % length
    angle = 2.0 * np.pi / length * phase
    upper = np.stack([np.cos(angle), -np.sin(angle)], axis=1)
    lower = np.stack([np.sin(angle), np.cos(angle)], axis=1)
    return np.stack([upper, lower])


def np_depth(length, count):
    phase = np.arange(length)[:, None] * np.arange(count)[None, :] % length
    angle = 2.0 * np.pi / length * phase
    return np.stack([np.cos(angle), -np.sin(angle)])


def iota(shape, axis):
    return lax.broadcasted_iota(jnp.int32, shape, axis)


def one_hot(rows, cols, row_of, col_of):
    return row_of(iota((rows, cols), 0)) == col_of(iota((rows, cols), 1))


def spread(weights, rows_first):
    first, second = weights.shape
    rows, cols = (second, first) if rows_first else (first, second)
    pick = one_hot(rows * SUB, rows, lambda r: r // SUB, lambda c: c).astype(F32).astype(BF16)
    lay = one_hot(cols * SUB, cols, lambda r: r // SUB, lambda c: c).astype(F32).astype(BF16)
    same = one_hot(rows * SUB, cols * SUB, lambda r: r % SUB, lambda c: c % SUB)
    result = []
    for part in halves(weights):
        tall = mul(pick, part, NT if rows_first else NN).astype(BF16)
        wide = mul(tall, lay, NT)
        result.append(jnp.where(same, wide, 0.0).astype(BF16))
    return result


class Place:
    def __init__(self, px, py):
        self.px, self.py = px, py
        self.p = lax.axis_index("px")
        self.q = lax.axis_index("py")
        self.core = lax.rem(self.q, 2)
        self.side = self.q // 2
        self.mate = {"py": self.q + 1 - 2 * self.core}
        self.cross = {"py": lax.rem(self.q + 2, py)}

    def row_peer(self, step):
        return lax.rem(self.p + step, self.px)

    def col_peer(self, step):
        return lax.rem(self.q + step, self.py)

    def greet(self):
        barrier = pltpu.get_barrier_semaphore()
        for step in range(1, self.px):
            pl.semaphore_signal(barrier, inc=1, device_id={"px": self.row_peer(step)}, device_id_type=MESH)
        for step in range(1, self.py):
            pl.semaphore_signal(barrier, inc=1, device_id={"py": self.col_peer(step)}, device_id_type=MESH)
        pl.semaphore_wait(barrier, self.px + self.py - 2)


def remote(src, dst, send, recv, device):
    return pltpu.make_async_remote_copy(
        src_ref=src, dst_ref=dst, send_sem=send, recv_sem=recv, device_id=device, device_id_type=MESH,
    )


def forward_kernel(px, py, flow_ref, cot_ref, ty_ref, win_ref, wout_ref, tz_ref, tx_ref, out_ref,
                   tile, kron, lines_h, lines_l, modes_h, modes_l, ty, summed, from_mate, to_cross,
                   from_cross, to_row, gathered, load_sem, table_sem, mate_send, mate_recv,
                   cross_send, cross_recv, row_send, row_recv):
    here = Place(px, py)
    steps, channels, group, cols, depth = tile.shape
    tiles = steps // 2
    ranks = win_ref.shape[1]
    packs = ranks // 4
    loads = []
    for t in range(steps):
        source = flow_ref if t < tiles else cot_ref
        loads.append(pltpu.make_async_copy(
            source.at[:, pl.ds((t % tiles) * group, group)], tile.at[t], load_sem.at[t]))
        loads[t].start()
    table = pltpu.make_async_copy(ty_ref.at[here.q], ty, table_sem)
    table.start()
    here.greet()
    for f, weight in enumerate((win_ref, wout_ref)):
        high, low = spread(weight[...], True)
        kron[f, :ranks * SUB] = high
        kron[f, ranks * SUB:] = low
    table.wait()

    def mate_copies(t):
        return [remote(summed.at[t, 2 * s + 1 - here.core], from_mate.at[t, s],
                       mate_send.at[t, s], mate_recv.at[t, s], here.mate) for s in range(2)]

    def cross_copy(t):
        return remote(to_cross.at[t], from_cross.at[t], cross_send.at[t], cross_recv.at[t], here.cross)

    def row_copy(t, step):
        return remote(to_row.at[t, here.row_peer(step)], gathered.at[t // tiles, here.p, lax.rem(t, tiles)],
                      row_send.at[t, step], row_recv.at[t, step], {"px": here.row_peer(step)})

    def compute(t):
        f = t // tiles

        def lift(x, carry):
            sides = [tile[t, :, x, h * SUB:(h + 1) * SUB, :].reshape(channels * SUB, depth)
                     for h in range(cols // SUB)]
            both = mul(kron[f], jnp.concatenate(sides, axis=1))
            high, low = halves(both[:ranks * SUB] + both[ranks * SUB:])
            for a in range(ranks):
                for h in range(cols // SUB):
                    row = pl.multiple_of(x * (packs * cols) + (a // 4) * cols + h * SUB, SUB)
                    spot = (pl.ds(row, SUB), slice((a % 4) * depth, (a % 4 + 1) * depth))
                    part = (slice(a * SUB, (a + 1) * SUB), slice(h * depth, (h + 1) * depth))
                    lines_h[spot] = high[part]
                    lines_l[spot] = low[part]
            return carry

        lax.fori_loop(0, group, lift, 0)
        modes = mul3((lines_h[...], lines_l[...]), (tz_ref[0], tz_ref[1]))
        high, low = halves(modes)
        for x in range(group):
            for a in range(packs):
                for p in range(2):
                    spot = (slice((x * 2 + p) * cols, (x * 2 + p + 1) * cols), slice(a * LANES, (a + 1) * LANES))
                    part = (slice((x * packs + a) * cols, (x * packs + a + 1) * cols),
                            slice(p * LANES, (p + 1) * LANES))
                    modes_h[spot] = high[part]
                    modes_l[spot] = low[part]
        total = mul3((ty[0], ty[1]), (modes_h[...], modes_l[...]))
        summed[t] = total.reshape(summed.shape[1:])

    def body(t, carry):
        @pl.when(t < steps)
        def _():
            pltpu.make_async_copy(flow_ref.at[:, pl.ds(0, group)], tile.at[t], load_sem.at[t]).wait()
            compute(t)
            for copy in mate_copies(t):
                copy.start()

        @pl.when((t >= 1) & (t < steps + 1))
        def _():
            u = t - 1
            for copy in mate_copies(u):
                copy.wait_recv()
            to_cross[u] = summed[u, 2 * (1 - here.side) + here.core] + from_mate[u, 1 - here.side]
            cross_copy(u).start()

        @pl.when(t >= 3)
        def _():
            u = t - 3
            cross_copy(u).wait_recv()
            whole = summed[u, 2 * here.side + here.core] + from_mate[u, here.side] + from_cross[u]
            to_row[u] = whole
            for step in range(1, px):
                row_copy(u, step).start()
            gathered[u // tiles, here.p, lax.rem(u, tiles)] = to_row[u, here.p]

        return carry

    lax.fori_loop(0, steps + 3, body, 0)
    for f in range(2):
        for t in range(f * tiles, (f + 1) * tiles):
            for step in range(1, px):
                row_copy(t, step).wait_recv()
        lines = gathered[f].reshape(-1, packs * LANES)
        out_ref[f] = mul3((tx_ref[0], tx_ref[1]), halves(lines))

    def drain(t, carry):
        for copy in mate_copies(t):
            copy.wait_send()
        cross_copy(t).wait_send()
        for step in range(1, px):
            row_copy(t, step).wait_send()
        return carry

    lax.fori_loop(0, steps, drain, 0)


def mix_kernel(px, py, second_smem, spectra_ref, core_ref, first_ref, third_ref, scale_ref,
               mixed_ref, part_ref, small_ref, bk_ref, gk_ref, kernel_rows):
    k = lax.axis_index("py") * px + lax.axis_index("px")
    r2, rows, width = core_ref.shape
    m1, r1 = first_ref.shape
    m3, r3 = third_ref.shape
    packs = spectra_ref.shape[2] // LANES
    ranks = 4 * packs
    core = second_smem[k, 0] * core_ref[0]
    for s in range(1, r2):
        core = core + second_smem[k, s] * core_ref[s]
    pick = one_hot(width, r3, lambda r: r % r3, lambda c: c).astype(F32)
    small = exact(pick, third_ref[...], NT)
    wide = jnp.concatenate([small] * 4, axis=1)
    same = one_hot(width, LANES, lambda r: r // r3, lambda c: c // m3)
    third = jnp.where(same, wide, 0.0)
    heavy = exact(core, third)
    kernel_rows[...] = heavy
    group_of = iota((m1, LANES), 1) // m3
    columns = [jnp.broadcast_to(first_ref[:, r:r + 1], (m1, LANES)) for r in range(r1)]
    lift = [[spectra_ref[0, p * m1:(p + 1) * m1, a * LANES:(a + 1) * LANES] for a in range(packs)]
            for p in range(2)]
    scale = scale_ref[...]
    for p in range(2):
        for a in range(packs):
            bk_ref[p, a] = spectra_ref[1, p * m1:(p + 1) * m1, a * LANES:(a + 1) * LANES] * scale
    mixed_ref[...] = jnp.zeros_like(mixed_ref)

    def around(v):
        v = v + pltpu.roll(v, 64, 1)
        return v + pltpu.roll(v, 32, 1)

    def body(b, carry):
        mine = group_of == lax.rem(b, 4)
        kern = []
        for a in range(packs):
            block = kernel_rows[pl.ds(pl.multiple_of((b * packs + a) * r1, r1), r1), :]
            total = columns[0] * block[0:1]
            for r in range(1, r1):
                total = total + columns[r] * block[r:r + 1]
            kern.append(total)
        grad = [None] * packs
        for p in range(2):
            back = around(jnp.where(mine, bk_ref[p, b // 4], 0.0))
            sums = kern[0] * lift[p][0]
            for a in range(1, packs):
                sums = sums + kern[a] * lift[p][a]
            sums = jnp.where(mine, around(sums), 0.0)
            for a in range(packs):
                cell = (0, slice(p * m1, (p + 1) * m1), slice(a * LANES, (a + 1) * LANES))
                mixed_ref[cell] += kern[a] * back
                term = back * lift[p][a]
                grad[a] = term if p == 0 else grad[a] + term
            lanes = pl.ds(pl.multiple_of((b // 4) * LANES, LANES), LANES)
            mixed_ref[1, pl.ds(p * m1, m1), lanes] += sums
        for a in range(packs):
            gk_ref[:, pl.ds(pl.multiple_of((b * packs + a) * LANES, LANES), LANES)] = grad[a]
        return carry

    lax.fori_loop(0, ranks, body, 0)
    for p in range(2):
        for a in range(packs):
            cell = (1, slice(p * m1, (p + 1) * m1), slice(a * LANES, (a + 1) * LANES))
            mixed_ref[cell] = mixed_ref[cell] * scale
    count = rows // r1
    grads = gk_ref[...]
    spread_rows = jnp.concatenate([heavy[i * r1:(i + 1) * r1] for i in range(count)], axis=1)
    grad_first = exact(grads, spread_rows, NT)
    thin = exact(first_ref[...], grads, TN)
    tall = jnp.concatenate([thin[:, i * LANES:(i + 1) * LANES] for i in range(count)], axis=0)
    lay = one_hot(LANES, r3, lambda r: r % r3, lambda c: c).astype(F32)
    tiled = jnp.concatenate([third_ref[...]] * 4, axis=0)
    square = exact(tiled, lay, NT)
    match = one_hot(LANES, LANES, lambda r: r // m3, lambda c: (c // r3) % 4)
    part = exact(tall, jnp.where(match, square, 0.0))
    part_ref[...] = part
    cross = exact(tall, core, TN)
    cross = jnp.where(one_hot(LANES, width, lambda r: r // m3, lambda c: c // r3), cross, 0.0)
    cross = cross[:m3] + cross[m3:2 * m3] + cross[2 * m3:3 * m3] + cross[3 * m3:]
    shift = one_hot(width, LANES, lambda r: r % r3 + r1, lambda c: c).astype(F32)
    total = exact(cross, shift)
    total = total + exact(grad_first, one_hot(r1, LANES, lambda r: r, lambda c: c).astype(F32))
    lane = iota((m3, LANES), 1)
    row = iota((m3, LANES), 0)
    for s in range(r2):
        value = jnp.sum(core_ref[s] * part[:, :width])
        total = total + jnp.where((lane == r1 + r3 + s) & (row == k), value, 0.0)
    small_ref[...] = total


def backward_kernel(px, py, flow_ref, cot_ref, ty_ref, modes_ref, part_ref, small_ref, second_ref,
                    wout_ref, tx_ref, tz_ref, out_ref, core_out, small_out, pair_out,
                    tile, kron, to_row, blocks, ty, lines_h, lines_l, real_h, real_l, field, totals,
                    ranks_in, ranks_sum, ranks_col, core_all, small_row, small_sum, small_col,
                    pair_row, pair_sum, pair_col,
                    load_sem, table_sem, out_sem, row_send, row_recv, cross_send, cross_recv,
                    mate_send, mate_recv, rs_send, rs_recv, cs_send, cs_recv, ag_send, ag_recv,
                    bg_send, bg_recv, sr_send, sr_recv, sc_send, sc_recv, pr_send, pr_recv, pc_send, pc_recv):
    here = Place(px, py)
    steps, channels, group, cols, depth = tile.shape
    tiles = steps // 2
    ranks = wout_ref.shape[1]
    packs = ranks // 4
    q, p = here.q, here.p
    for t in range(steps):
        source = flow_ref if t < tiles else cot_ref
        pltpu.make_async_copy(
            source.at[:, pl.ds((t % tiles) * group, group)], tile.at[t], load_sem.at[t]).start()
    table = pltpu.make_async_copy(ty_ref.at[here.q], ty, table_sem)
    table.start()
    here.greet()
    share = part_ref.shape[0] // px
    piece = share // py

    def rs_copy(step):
        to = here.row_peer(step)
        return remote(part_ref.at[pl.ds(to * share, share)], ranks_in.at[p], rs_send.at[step], rs_recv.at[step],
                      {"px": to})

    def cs_copy(step):
        to = here.col_peer(step)
        return remote(ranks_sum.at[to], ranks_col.at[q], cs_send.at[step], cs_recv.at[step], {"py": to})

    def ag_copy(step):
        return remote(core_all.at[p, q], core_all.at[p, q], ag_send.at[step], ag_recv.at[step],
                      {"px": here.row_peer(step)})

    def bg_copy(step):
        return remote(core_all.at[:, q], core_all.at[:, q], bg_send.at[step], bg_recv.at[step],
                      {"py": here.col_peer(step)})

    def sr_copy(step):
        return remote(small_ref, small_row.at[p], sr_send.at[step], sr_recv.at[step],
                      {"px": here.row_peer(step)})

    def sc_copy(step):
        return remote(small_sum, small_col.at[q], sc_send.at[step], sc_recv.at[step],
                      {"py": here.col_peer(step)})

    def pr_copy(step):
        return remote(pair_sum.at[0], pair_row.at[p], pr_send.at[step], pr_recv.at[step],
                      {"px": here.row_peer(step)})

    def pc_copy(step):
        return remote(pair_sum.at[1], pair_col.at[q], pc_send.at[step], pc_recv.at[step],
                      {"py": here.col_peer(step)})

    def row_copy(t, step):
        to = here.row_peer(step)
        return remote(to_row.at[t // tiles, to, lax.rem(t, tiles)], blocks.at[t, q, p],
                      row_send.at[t, step], row_recv.at[t, step], {"px": to})

    def cross_copy(t):
        return remote(blocks.at[t, q], blocks.at[t, q], cross_send.at[t], cross_recv.at[t], here.cross)

    def mate_copy(t, s):
        quarter = q if s == 0 else lax.rem(q + 2, py)
        return remote(blocks.at[t, quarter], blocks.at[t, quarter],
                      mate_send.at[t, s], mate_recv.at[t, s], here.mate)

    for f in range(2):
        lines = mul3((tx_ref[0], tx_ref[1]), halves(modes_ref[f]))
        to_row[f] = lines.reshape(to_row.shape[1:])
        for t in range(f * tiles, (f + 1) * tiles):
            for step in range(1, px):
                row_copy(t, step).start()
            blocks[t, q, p] = to_row[f, p, t - f * tiles]
    for step in range(1, px):
        rs_copy(step).start()
        sr_copy(step).start()
    ranks_in[p] = part_ref[pl.ds(pl.multiple_of(p * share, share), share), :]
    small_row[p] = small_ref[...]
    high, low = spread(wout_ref[...], False)
    kron[0] = high
    kron[1] = low
    totals[...] = jnp.zeros_like(totals)
    table.wait()

    def place(t):
        high, low = halves(blocks[t].reshape(-1, packs * LANES))
        modes = mul3((ty[0], ty[1]), (high, low))
        high, low = halves(modes)
        for x in range(group):
            for a in range(packs):
                for o in range(2):
                    part = (slice((x * 2 + o) * cols, (x * 2 + o + 1) * cols), slice(a * LANES, (a + 1) * LANES))
                    spot = (slice((x * packs + a) * cols, (x * packs + a + 1) * cols),
                            slice(o * LANES, (o + 1) * LANES))
                    lines_h[spot] = high[part]
                    lines_l[spot] = low[part]
        real = mul3((lines_h[...], lines_l[...]), (tz_ref[0], tz_ref[1]))
        high, low = halves(real)
        for x in range(group):
            for a in range(ranks):
                for h in range(cols // SUB):
                    row = (x * packs + a // 4) * cols + h * SUB
                    part = (slice(row, row + SUB), slice((a % 4) * depth, (a % 4 + 1) * depth))
                    spot = (x, slice(a * SUB, (a + 1) * SUB), slice(h * depth, (h + 1) * depth))
                    real_h[spot] = high[part]
                    real_l[spot] = low[part]

    def outer(t):
        def one(x, carry):
            sides = [tile[t, :, x, h * SUB:(h + 1) * SUB, :].reshape(channels * SUB, depth)
                     for h in range(cols // SUB)]
            cells = jnp.concatenate(sides, axis=1)
            totals[t // tiles] += mul(cells, real_h[x], NT) + mul(cells, real_l[x], NT)
            return carry

        lax.fori_loop(0, group, one, 0)

    def emit(t):
        g = t - tiles

        def one(x, carry):
            both = mul3((kron[0], kron[1]), (real_h[x], real_l[x])).astype(BF16)
            for h in range(cols // SUB):
                field[g, :, x, h * SUB:(h + 1) * SUB, :] = both[:, h * depth:(h + 1) * depth].reshape(
                    channels, SUB, depth)
            return carry

        lax.fori_loop(0, group, one, 0)
        out_copy(g).start()

    def out_copy(g):
        return pltpu.make_async_copy(field.at[g], out_ref.at[:, pl.ds(g * group, group)], out_sem.at[g])

    def body(i, carry):
        @pl.when(i < steps)
        def _():
            for step in range(1, px):
                row_copy(i, step).wait_recv()
            cross_copy(i).start()
            mate_copy(i, 0).start()

        @pl.when((i >= 2) & (i < steps + 2))
        def _():
            cross_copy(i - 2).wait_recv()
            mate_copy(i - 2, 1).start()

        @pl.when(i >= 3)
        def _():
            t = i - 3
            for s in range(2):
                mate_copy(t, s).wait_recv()
            pltpu.make_async_copy(flow_ref.at[:, pl.ds(0, group)], tile.at[t], load_sem.at[t]).wait()
            place(t)
            outer(t)

        @pl.when(i >= 3 + tiles)
        def _():
            emit(i - 3)

        @pl.when(i == 4)
        def _():
            for step in range(1, px):
                rs_copy(step).wait_recv()
                sr_copy(step).wait_recv()
            half = second_ref.shape[2] // LANES
            mine = second_ref[q]
            sums = []
            for o in range(half):
                total = None
                for s in range(px):
                    weight = mine[s:s + 1, o * LANES:(o + 1) * LANES]
                    term = ranks_in[s] * weight
                    total = term if total is None else total + term
                sums.append(total)
            ranks_sum[...] = jnp.concatenate(sums, axis=1).reshape(ranks_sum.shape)
            total = small_row[0]
            for s in range(1, px):
                total = total + small_row[s]
            small_sum[...] = total
            small_col[q] = total
            ranks_col[q] = ranks_sum[q]
            for step in range(1, py):
                cs_copy(step).start()
                sc_copy(step).start()

        @pl.when(i == 6)
        def _():
            for step in range(1, py):
                cs_copy(step).wait_recv()
                sc_copy(step).wait_recv()
            total = ranks_col[0]
            small = small_col[0]
            for s in range(1, py):
                total = total + ranks_col[s]
                small = small + small_col[s]
            core_all[p, q] = total
            small_out[...] = small
            for step in range(1, px):
                ag_copy(step).start()

        @pl.when(i == 8)
        def _():
            for step in range(1, px):
                ag_copy(step).wait_recv()
            for step in range(1, py):
                bg_copy(step).start()

        return carry

    lax.fori_loop(0, steps + 3, body, 0)
    keep = one_hot(channels * SUB, ranks * SUB, lambda r: r % SUB, lambda c: c % SUB)
    pair = None
    for f in range(2):
        grid = jnp.where(keep, totals[f], 0.0).reshape(channels, SUB, ranks * SUB).sum(axis=1)
        for i in range(channels // SUB):
            base = (2 * i + f) * ranks
            pick = one_hot(ranks * SUB, LANES, lambda r: r // SUB + base, lambda c: c).astype(F32)
            term = exact(grid[i * SUB:(i + 1) * SUB], pick)
            pair = term if pair is None else pair + term
    pair_sum[0] = pair
    pair_row[p] = pair
    for step in range(1, px):
        pr_copy(step).start()
    for step in range(1, py):
        bg_copy(step).wait_recv()
    core_out[...] = core_all[...]
    for step in range(1, px):
        pr_copy(step).wait_recv()
    total = pair_row[0]
    for s in range(1, px):
        total = total + pair_row[s]
    pair_sum[1] = total
    pair_col[q] = total
    for step in range(1, py):
        pc_copy(step).start()
    for step in range(1, py):
        pc_copy(step).wait_recv()
    total = pair_col[0]
    for s in range(1, py):
        total = total + pair_col[s]
    pair_out[...] = total

    def drain(t, carry):
        for step in range(1, px):
            row_copy(t, step).wait_send()
        cross_copy(t).wait_send()
        for s in range(2):
            mate_copy(t, s).wait_send()
        return carry

    lax.fori_loop(0, steps, drain, 0)
    for step in range(1, px):
        for copy in (rs_copy, sr_copy, ag_copy, pr_copy):
            copy(step).wait_send()
    for step in range(1, py):
        for copy in (cs_copy, sc_copy, bg_copy, pc_copy):
            copy(step).wait_send()
    for g in range(tiles):
        out_copy(g).wait()


def fast_shards(px, py, flow_field, cotangent, tucker_core, in_factor, out_factor,
                first_factor, second_factor, third_factor):
    channels, rows, cols, depth = flow_field.shape
    ri, ro, r1, r2, r3 = tucker_core.shape
    group = 2 * LANES // (2 * cols)
    tiles = rows // group
    steps = 2 * tiles
    packs = ri // 4
    wide = packs * LANES
    keep = px
    inverse_count = 1.0 / (NX * NY * NZ)

    small = np_depth(NZ, M3)
    tz = np.einsum("st,pzm->szptm", np.eye(4), small).reshape(4 * depth, 2 * 4 * M3)
    turn = np_turn(M2, NY).reshape(2, py, cols, 2, py, keep)
    ty = np.einsum("pdyoqk,xw->dqkxowpy", turn, np.eye(group))
    ty = ty.reshape(py, py * keep * group * 2, group * 2 * cols)
    turn = np_turn(M1, NX).reshape(2, NX, 2, M1)
    tx = turn.transpose(2, 3, 1, 0).reshape(2 * M1, NX * 2)
    tz_f, tz_b = np_halves(tz), np_halves(tz.T)
    ty_f = np_halves(ty).swapaxes(0, 1)
    ty_b = np_halves(ty.swapaxes(1, 2)).swapaxes(0, 1)
    tx_f, tx_b = np_halves(tx), np_halves(tx.T)
    weight = np.where(np.arange(M3) == 0, 1.0, 2.0) * inverse_count
    scale = jnp.asarray(np.tile(weight, 4)[None, :].astype(np.float32))

    vmem = pl.BlockSpec(memory_space=pltpu.VMEM)
    anywhere = pl.BlockSpec(memory_space=pl.ANY)
    shape = jax.ShapeDtypeStruct
    dma = pltpu.SemaphoreType.DMA

    def params(number):
        return pltpu.CompilerParams(
            vmem_limit_bytes=VMEM_LIMIT, collective_id=number, has_side_effects=True)

    def cost(flops):
        return pl.CostEstimate(flops=flops, bytes_accessed=10 ** 7, transcendentals=0)

    lines = group * packs * cols
    block = (keep, 2 * group, wide)
    spectra = pl.pallas_call(
        functools.partial(forward_kernel, px, py),
        out_shape=shape((2, 2 * M1, wide), F32),
        in_specs=[anywhere, anywhere, anywhere, vmem, vmem, vmem, vmem],
        out_specs=vmem,
        scratch_shapes=[
            pltpu.VMEM((steps, channels, group, cols, depth), BF16),
            pltpu.VMEM((2, 2 * ri * SUB, channels * SUB), BF16),
            pltpu.VMEM((lines, 4 * depth), BF16), pltpu.VMEM((lines, 4 * depth), BF16),
            pltpu.VMEM((group * 2 * cols, wide), BF16), pltpu.VMEM((group * 2 * cols, wide), BF16),
            pltpu.VMEM(ty_f.shape[1:], BF16),
            pltpu.VMEM((steps, py) + block, F32),
            pltpu.VMEM((steps, 2) + block, F32),
            pltpu.VMEM((steps,) + block, F32),
            pltpu.VMEM((steps,) + block, F32),
            pltpu.VMEM((steps,) + block, F32),
            pltpu.VMEM((2, px, tiles, 2 * group, wide), F32),
            dma((steps,)), dma,
            dma((steps, 2)), dma((steps, 2)), dma((steps,)), dma((steps,)),
            dma((steps, px)), dma((steps, px)),
        ],
        compiler_params=params(0), cost_estimate=cost(10 ** 10),
    )(flow_field, cotangent, jnp.asarray(ty_f), in_factor, out_factor, jnp.asarray(tz_f), jnp.asarray(tx_f))

    core = tucker_core.reshape(packs, 4, ro, r1, r2, r3).transpose(4, 2, 0, 3, 1, 5)
    core = core.reshape(r2, ro * packs * r1, 4 * r3)
    count = ro * packs * r1
    smem = pl.BlockSpec(memory_space=pltpu.SMEM)
    modes, part, little = pl.pallas_call(
        functools.partial(mix_kernel, px, py),
        out_shape=(shape((2, 2 * M1, wide), F32), shape((count, LANES), F32), shape((M3, LANES), F32)),
        in_specs=[smem, vmem, vmem, vmem, vmem, vmem], out_specs=(vmem,) * 3,
        scratch_shapes=[
            pltpu.VMEM((2, packs, M1, LANES), F32),
            pltpu.VMEM((M1, ro * wide), F32),
            pltpu.VMEM((count, LANES), F32),
        ],
        compiler_params=pltpu.CompilerParams(vmem_limit_bytes=VMEM_LIMIT), cost_estimate=cost(10 ** 9),
    )(second_factor, spectra, core, first_factor, third_factor, scale)

    spread_second = jnp.repeat(second_factor, LANES // 4, axis=1).reshape(py, px, -1)
    share, piece = count // px, count // px // py
    span = spread_second.shape[2]
    out, core_sum, little, pair = pl.pallas_call(
        functools.partial(backward_kernel, px, py),
        out_shape=(
            shape(flow_field.shape, BF16), shape((px, py, piece, span), F32),
            shape((M3, LANES), F32), shape((SUB, LANES), F32),
        ),
        in_specs=[anywhere, anywhere, anywhere] + [vmem] * 7,
        out_specs=(anywhere, vmem, vmem, vmem),
        scratch_shapes=[
            pltpu.VMEM((steps, channels, group, cols, depth), BF16),
            pltpu.VMEM((2, channels * SUB, ro * SUB), BF16),
            pltpu.VMEM((2, px, tiles, 2 * group, wide), F32),
            pltpu.VMEM((steps, py) + block, F32),
            pltpu.VMEM(ty_b.shape[1:], BF16),
            pltpu.VMEM((lines, 2 * LANES), BF16), pltpu.VMEM((lines, 2 * LANES), BF16),
            pltpu.VMEM((group, ri * SUB, cols // SUB * depth), BF16),
            pltpu.VMEM((group, ri * SUB, cols // SUB * depth), BF16),
            pltpu.VMEM((tiles, channels, group, cols, depth), BF16),
            pltpu.VMEM((2, channels * SUB, ri * SUB), F32),
            pltpu.VMEM((px, share, LANES), F32), pltpu.VMEM((py, piece, span), F32),
            pltpu.VMEM((py, piece, span), F32), pltpu.VMEM((px, py, piece, span), F32),
            pltpu.VMEM((px, M3, LANES), F32), pltpu.VMEM((M3, LANES), F32), pltpu.VMEM((py, M3, LANES), F32),
            pltpu.VMEM((px, SUB, LANES), F32), pltpu.VMEM((2, SUB, LANES), F32), pltpu.VMEM((py, SUB, LANES), F32),
            dma((steps,)), dma, dma((tiles,)),
            dma((steps, px)), dma((steps, px)), dma((steps,)), dma((steps,)),
            dma((steps, 2)), dma((steps, 2)),
            dma((px,)), dma((px,)), dma((py,)), dma((py,)), dma((px,)), dma((px,)), dma((py,)), dma((py,)),
            dma((px,)), dma((px,)), dma((py,)), dma((py,)), dma((px,)), dma((px,)), dma((py,)), dma((py,)),
        ],
        compiler_params=params(1), cost_estimate=cost(10 ** 10),
    )(flow_field, cotangent, jnp.asarray(ty_b), modes, part, little, spread_second, out_factor,
      jnp.asarray(tx_b), jnp.asarray(tz_b))

    core_grad = core_sum.reshape(ro, packs, r1, r2, 4, r3).transpose(1, 4, 0, 2, 3, 5).reshape(tucker_core.shape)
    pair = pair.reshape(SUB, channels // SUB, 2, ri).transpose(2, 1, 0, 3).reshape(2, channels, ri)
    return (out, core_grad, pair[0], pair[1], little[:, :r1],
            little[:, r1 + r3:r1 + r3 + r2], little[:, r1:r1 + r3])


def solution(mesh):
    px, py = mesh.shape["px"], mesh.shape["py"]
    rows, cols = NX // px, NY // py
    fits = py == 4 and px * py == M2 and cols == 32 and rows % 4 == 0 and NZ == LANES
    fits = fits and M1 == 32 and M3 == 32
    body = functools.partial(fast_shards, px, py) if fits else shards
    return jax.shard_map(
        body,
        mesh=mesh,
        in_specs=(
            P(None, "px", "py", None),
            P(None, "px", "py", None),
            P(),
            P(),
            P(),
            P(),
            P(),
            P(),
        ),
        out_specs=(P(None, "px", "py", None), P(), P(), P(), P(), P(), P()),
        check_vma=False,
    )
```

profile of v0, /device:TPU:0, one launch (start us, length us, event | category | flops | bytes accessed | tf_op | source)
XLA Modules:
  0.0 199.4 jit_solution(12679522807467710570)
XLA Ops:
  0.6 1.4 copy.53.second_smem
  2.0 1.4 copy.50.win_ref
  3.4 1.4 copy.51.wout_ref
  4.8 51.2 %shard_map.198.spectra_ref = f32[2,64,512]{2,1,0:T(8,128)} custom-call(bf16[64,16,32,128]{3,2,1,0:T(8,128)(2,1)} %flow_ref.3, bf16[64,16,32,128]{3,2,1,0:T(8,128)(2,1)} %cot_ref.3, bf16[4,2,256,256]{3,2,1,0:T(8,128)(2,1)} %constant.15.clone.ty_ref, f32[64,16]{1,0:T(8,128)} %copy.50.win_ref, f32[64,16]{1,0:T(8,128)} %copy.51.wout_ref, ...), custom_call_target="tpu_custom_call" | custom-call | flops 10000000000 | bytes 10000000 | tf_op jit(solution)/shard_map/pallas_call | solution.py:756
  56.0 8.4 %copy.52 = f32[4,4,16,8,8,8]{3,0,2,5,1,4:T(4,128)} copy(f32[4,4,16,8,8,8]{2,5,4,3,1,0:T(8,128)} %bitcast.15) | data formatting | bytes 1048576 | tf_op jit(solution)/shard_map/reshape | solution.py:780
  64.5 0.0 copy-start.3
  64.5 11.5 %reshape.35 = f32[8,512,32]{1,2,0:T(8,128)S(1)} reshape(f32[8,16,4,8,4,8]{3,2,1,5,4,0:T(4,128)} %bitcast.14) | data formatting | bytes 1048576 | tf_op jit(solution)/shard_map/reshape | solution.py:781
  76.0 1.9 copy.54.core_ref
  78.0 0.0 copy-done.3
  78.0 0.7 copy.55.first_ref
  78.6 0.0 copy-done.4
  78.6 0.7 copy.56.third_ref
  79.3 8.8 %shard_map.199 = (f32[2,64,512]{2,1,0:T(8,128)}, f32[512,128]{1,0:T(8,128)}, f32[32,128]{1,0:T(8,128)}) custom-call(f32[32,8]{1,0:T(8,128)} %copy.53.second_smem, f32[2,64,512]{2,1,0:T(8,128)} %shard_map.198.spectra_ref, f32[8,512,32]{2,1,0:T(8,128)} %copy.54.core_ref, f32[32,8]{1,0:T(8,128)} %copy.55.first_ref, f32[32,8]{1,0:T(8,128)} %copy.56.third_ref, ...), custom_call_target="tpu_custom_call" | custom-call | flops 1000000000 | bytes 10000000 | tf_op jit(solution)/shard_map/pallas_call | solution.py:784
  88.2 0.0 copy-done.1
  88.2 0.1 broadcast_in_dim.3
  88.3 0.7 reshape_reshape.3.second_ref
  89.0 75.9 %shard_map.200 = (bf16[64,16,32,128]{3,2,1,0:T(8,128)(2,1)}, f32[8,4,16,256]{3,2,1,0:T(8,128)}, f32[32,128]{1,0:T(8,128)}, f32[16,128]{1,0:T(8,128)}) custom-call(bf16[64,16,32,128]{3,2,1,0:T(8,128)(2,1)} %flow_ref.3, bf16[64,16,32,128]{3,2,1,0:T(8,128)(2,1)} %cot_ref.3, bf16[4,2,256,256]{3,2,1,0:T(8,128)(2,1)} %constant.18.clone.ty_ref, ...), custom_call_target="tpu_custom_call" | custom-call | flops 10000000000 | bytes 10000000 | tf_op jit(solution)/shard_map/pallas_call | solution.py:799
  164.9 12.2 %reshape.36 = f32[16,4,8,8,4,8]{5,4,3,2,1,0:T(4,128)} reshape(f32[8,4,16,256]{3,2,1,0:T(8,128)} %get-tuple-element.18) | data formatting | bytes 1048576 | tf_op jit(solution)/shard_map/reshape | solution.py:832
  177.1 9.0 %copy.59 = f32[4,4,16,8,8,8]{2,5,4,3,1,0:T(8,128)} copy(f32[4,4,16,8,8,8]{5,1,4,3,0,2:T(4,128)} %bitcast.13) | data formatting | bytes 1048576 | tf_op jit(solution)/shard_map/transpose | solution.py:832
  186.1 0.0 copy-done.2
  186.1 0.1 reshape.38
  186.3 0.1 fusion
  186.3 0.1 copy.60
  186.4 0.7 squeeze.6
  187.1 0.1 copy.61
  187.2 0.7 squeeze.7
  187.9 0.0 copy-done
  187.9 0.1 fusion.1
  188.0 0.7 copy.62
  188.6 0.7 copy.63
  189.3 0.7 copy.64
  189.9 9.4 %copy.66 = bf16[64,16,32,128]{3,2,1,0:T(8,128)(2,1)} copy(bf16[64,16,32,128]{3,2,1,0:T(8,128)(2,1)} %get-tuple-element.54) | data formatting | bytes 16777216
  (4 shorter events, 0.0 us)
Async XLA Ops:
  64.5 13.5 %copy-start.3 = (f32[32,8]{0,1:T(8,128)S(1)}, f32[32,8]{0,1:T(8,128)}, u32[]{:S(2)}) copy-start(f32[32,8]{0,1:T(8,128)} %param.20) | copy-start | bytes 3076
  64.5 14.2 %copy-start.4 = (f32[32,8]{0,1:T(8,128)S(1)}, f32[32,8]{0,1:T(8,128)}, u32[]{:S(2)}) copy-start(f32[32,8]{0,1:T(8,128)} %param.22) | copy-start | bytes 3076
  64.5 23.7 %copy-start.1 = (f32[32,8]{1,0:T(8,128)S(1)}, f32[32,8]{1,0:T(8,128)}, u32[]{:S(2)}) copy-start(f32[32,8]{1,0:T(8,128)} %copy.53.second_smem) | copy-start | bytes 3076
  177.1 9.0 %copy-start.2 = (f32[16,128]{1,0:T(8,128)S(1)}, f32[16,128]{1,0:T(8,128)}, u32[]{:S(2)}) copy-start(f32[16,128]{1,0:T(8,128)} %get-tuple-element.19) | copy-start | bytes 24580
  177.1 10.8 %copy-start = (f32[32,128]{1,0:T(8,128)S(1)}, f32[32,128]{1,0:T(8,128)}, u32[]{:S(2)}) copy-start(f32[32,128]{1,0:T(8,128)} %get-tuple-element.20) | copy-start | bytes 49156
where the time goes:
time: 200 us; the launch traced here: 199 us
  Pallas kernels  136 us (68%)
  local copies, waits for them, and re-layouts  62.6 us (31%)
    pallas_call x1, Pallas kernels, fast_shards(): pl.pallas_call(functools.partial(backward_kernel, px, py), out_shape=(sha...  75.9 us
    pallas_call x1, Pallas kernels, fast_shards(): pl.pallas_call(functools.partial(forward_kernel, px, py), out_shape=shape...  51.2 us
    unnamed x19, local copies, waits for them, and re-layouts  16.9 us
    reshape x2, local copies, waits for them, and re-layouts, fast_shards(): core = core.reshape(r2, ro * packs * r1, 4 * r3)  13.5 us
    reshape x1, local copies, waits for them, and re-layouts, fast_shards(): core_sum.reshape(ro, packs, r1, r2, 4, r3).transpose(1, 4, 0, 2, 3, 5)  12.2 us
    transpose x1, local copies, waits for them, and re-layouts, fast_shards(): core_sum.reshape(ro, packs, r1, r2, 4, r3).transpose(1, 4, 0, 2, 3, 5)  9.04 us
    pallas_call x1, Pallas kernels, fast_shards(): pl.pallas_call(functools.partial(mix_kernel, px, py), out_shape=(shape((2...  8.85 us
    reshape x1, local copies, waits for them, and re-layouts, fast_shards(): tucker_core.reshape(packs, 4, ro, r1, r2, r3).transpose(4, 2, 0, 3, 1, 5)  8.44 us

commit v1 on v0

v1 whole, which is shorter than its diff:
```python
import functools
import math

import jax
import jax.numpy as jnp
import numpy as np
from jax import lax
from jax.experimental import pallas as pl
from jax.experimental.pallas import tpu as pltpu
from jax.sharding import PartitionSpec as P

NX = 128
NY = 128
NZ = 128
M1 = 32
M2 = 32
M3 = 32


HIGHEST = lax.Precision.HIGHEST


def turn_table(count, length):
    position = jnp.arange(count)
    frequency = jnp.where(position < count // 2, position, position - count)
    cells_at = jnp.arange(length)
    phase = frequency[None, :] * cells_at[:, None] % length
    angle = 2.0 * math.pi / length * phase.astype(jnp.float32)
    cosine = jnp.cos(angle)
    sine = jnp.sin(angle)
    upper = jnp.stack([cosine, -sine], axis=1)
    lower = jnp.stack([sine, cosine], axis=1)
    return jnp.stack([upper, lower])


def depth_table(length, count):
    cells_at = jnp.arange(length)
    frequency = jnp.arange(count)
    phase = cells_at[:, None] * frequency[None, :] % length
    angle = 2.0 * math.pi / length * phase.astype(jnp.float32)
    return jnp.concatenate([jnp.cos(angle), -jnp.sin(angle)], axis=1)


def to_modes(fields, depth_tables):
    across = turn_table(M2, NY)
    along = turn_table(M1, NX)
    spectra = []
    for member, z_table in zip(fields, depth_tables):
        channels, rows_here, cols_here, depth_len = member.shape
        flat = jnp.dot(member.reshape(-1, depth_len), z_table, precision=HIGHEST)
        spectra.append(flat.reshape(channels, rows_here, cols_here, 2, M3))
    members = lax.all_to_all(tuple(spectra), "py", split_axis=4, concat_axis=2, tiled=True)
    lines = tuple(
        (jnp.einsum("cxypm,pyqk->cxqkm", member, across, precision=HIGHEST) for member in members)
    )
    members = (
        lax.all_to_all(lines[0], "px", split_axis=3, concat_axis=1, tiled=True),
        lax.all_to_all(lines[1], "px", split_axis=3, concat_axis=1, tiled=True),
    )
    return tuple(
        (jnp.einsum("cxpkm,pxqj->cqjkm", member, along, precision=HIGHEST) for member in members)
    )


def to_space(modes, depth_weights):
    across = turn_table(M2, NY)
    along = turn_table(M1, NX)
    depth_base = depth_table(NZ, M3).T.reshape(2, M3, NZ)
    lines = tuple(
        (jnp.einsum("cqjkm,pxqj->cpxkm", member, along, precision=HIGHEST) for member in modes)
    )
    members = (
        lax.all_to_all(lines[0], "px", split_axis=2, concat_axis=3, tiled=True),
        lax.all_to_all(lines[1], "px", split_axis=2, concat_axis=3, tiled=True),
    )
    columns = tuple(
        (jnp.einsum("cqxkm,pyqk->cpxym", member, across, precision=HIGHEST) for member in members)
    )
    members = (
        lax.all_to_all(columns[0], "py", split_axis=3, concat_axis=4, tiled=True),
        lax.all_to_all(columns[1], "py", split_axis=3, concat_axis=4, tiled=True),
    )
    return tuple(
        (
            jnp.einsum(
                "cpxyk,pkn->cxyn", member, depth_base * weight_row[None, :, None], precision=HIGHEST
            )
            for member, weight_row in zip(members, depth_weights)
        )
    )


def shards(
    flow_field,
    cotangent,
    tucker_core,
    in_factor,
    out_factor,
    first_factor,
    second_factor,
    third_factor,
):
    inverse_count = 1.0 / (NX * NY * NZ)
    weights = jnp.where(jnp.arange(M3) == 0, 1.0, 2.0).astype(jnp.float32)
    unit_weights = jnp.ones((M3,), jnp.float32)
    base_table = depth_table(NZ, M3)
    weighted_table = base_table * jnp.concatenate([weights, weights])[None, :]
    block_second = M2 // lax.axis_size("px")
    block_third = M3 // lax.axis_size("py")
    start_second = lax.axis_index("px") * block_second
    start_third = lax.axis_index("py") * block_third

    def build_kernel(core_arg, first_arg, second_arg, third_arg):
        second_rows = lax.dynamic_slice_in_dim(second_arg, start_second, block_second, 0)
        third_rows = lax.dynamic_slice_in_dim(third_arg, start_third, block_third, 0)
        partial_core = jnp.einsum("abrst,mt->abrsm", core_arg, third_rows, precision=HIGHEST)
        partial_core = jnp.einsum("abrsm,ks->abrkm", partial_core, second_rows, precision=HIGHEST)
        return jnp.einsum("abrkm,jr->abjkm", partial_core, first_arg, precision=HIGHEST)

    kernel, pullback = jax.vjp(build_kernel, tucker_core, first_factor, second_factor, third_factor)
    field_wide = flow_field.astype(jnp.float32)
    back_wide = cotangent.astype(jnp.float32)
    lifted_grid = jnp.einsum("cxyn,ca->axyn", field_wide, in_factor, precision=HIGHEST)
    back_grid = jnp.einsum("cxyn,cb->bxyn", back_wide, out_factor, precision=HIGHEST)
    lifted, back_mixed = to_modes((lifted_grid, back_grid), (base_table, weighted_table))
    back_mixed = back_mixed * inverse_count
    mixed = jnp.einsum("abjkm,apjkm->bpjkm", kernel, lifted, precision=HIGHEST)
    grad_kernel = jnp.einsum("bpjkm,apjkm->abjkm", back_mixed, lifted, precision=HIGHEST)
    back_lifted = jnp.einsum("abjkm,bpjkm->apjkm", kernel, back_mixed, precision=HIGHEST)
    mixed_grid, lifted_back = to_space((mixed, back_lifted), (weights, unit_weights))
    mixed_grid = mixed_grid * inverse_count
    output_field = jnp.einsum("ob,bxyn->oxyn", out_factor, mixed_grid, precision=HIGHEST).astype(
        jnp.bfloat16
    )
    grad_out = jnp.einsum("oxyn,bxyn->ob", back_wide, mixed_grid, precision=HIGHEST)
    grad_in = jnp.einsum("ixyn,axyn->ia", field_wide, lifted_back, precision=HIGHEST)
    grad_core, grad_first, grad_second, grad_third = pullback(grad_kernel)
    totals = lax.psum(
        (grad_core, grad_in, grad_out, grad_first, grad_second, grad_third), ("px", "py")
    )
    return (output_field, totals[0], totals[1], totals[2], totals[3], totals[4], totals[5])


BF16 = jnp.bfloat16
F32 = jnp.float32
NN = (((1,), (0,)), ((), ()))
NT = (((1,), (1,)), ((), ()))
TN = (((0,), (0,)), ((), ()))
MESH = pl.DeviceIdType.MESH
VMEM_LIMIT = 63 * 1024 * 1024
SUB = 16
LANES = 128


def mul(a, b, dims=NN):
    return lax.dot_general(a, b, dims, preferred_element_type=F32)


def exact(a, b, dims=NN):
    return lax.dot_general(a, b, dims, precision=HIGHEST, preferred_element_type=F32)


def halves(x):
    high = x.astype(BF16)
    return high, (x - high.astype(F32)).astype(BF16)


def mul3(a, b, dims=NN):
    (ah, al), (bh, bl) = a, b
    return mul(ah, bh, dims) + (mul(ah, bl, dims) + mul(al, bh, dims))


def np_halves(x):
    x = np.asarray(x, np.float32)
    high = x.astype(BF16)
    return np.stack([high, (x - high.astype(np.float32)).astype(BF16)])


def np_turn(count, length):
    position = np.arange(count)
    frequency = np.where(position < count // 2, position, position - count)
    phase = frequency[None, :] * np.arange(length)[:, None] % length
    angle = 2.0 * np.pi / length * phase
    upper = np.stack([np.cos(angle), -np.sin(angle)], axis=1)
    lower = np.stack([np.sin(angle), np.cos(angle)], axis=1)
    return np.stack([upper, lower])


def np_depth(length, count):
    phase = np.arange(length)[:, None] * np.arange(count)[None, :] % length
    angle = 2.0 * np.pi / length * phase
    return np.stack([np.cos(angle), -np.sin(angle)])


def iota(shape, axis):
    return lax.broadcasted_iota(jnp.int32, shape, axis)


def one_hot(rows, cols, row_of, col_of):
    return row_of(iota((rows, cols), 0)) == col_of(iota((rows, cols), 1))


def spread(weights, dims):
    rows, cols = weights.shape if dims == NN else weights.shape[::-1]
    pick = one_hot(rows * SUB, rows, lambda r: r // SUB, lambda c: c).astype(F32).astype(BF16)
    lay = one_hot(cols * SUB, cols, lambda r: r // SUB, lambda c: c).astype(F32).astype(BF16)
    same = one_hot(rows * SUB, cols * SUB, lambda r: r % SUB, lambda c: c % SUB)
    result = []
    for part in halves(weights):
        tall = mul(pick, part, dims).astype(BF16)
        wide = mul(tall, lay, NT)
        result.append(jnp.where(same, wide, 0.0).astype(BF16))
    return result


def unfold(row, count, width):
    tall = jnp.broadcast_to(row, (count, row.shape[1]))
    return pltpu.roll(tall, 0, 1, stride=width, stride_axis=0)


class Place:
    def __init__(self, px, py):
        self.px, self.py = px, py
        self.p = lax.axis_index("px")
        self.q = lax.axis_index("py")
        self.core = lax.rem(self.q, 2)
        self.side = self.q // 2
        self.mate = {"py": self.q + 1 - 2 * self.core}
        self.cross = {"py": lax.rem(self.q + 2, py)}

    def row_peer(self, step):
        return lax.rem(self.p + step, self.px)

    def col_peer(self, step):
        return lax.rem(self.q + step, self.py)

    def greet(self):
        barrier = pltpu.get_barrier_semaphore()
        for step in range(1, self.px):
            pl.semaphore_signal(barrier, inc=1, device_id={"px": self.row_peer(step)}, device_id_type=MESH)
        for step in range(1, self.py):
            pl.semaphore_signal(barrier, inc=1, device_id={"py": self.col_peer(step)}, device_id_type=MESH)

    def meet(self):
        pl.semaphore_wait(pltpu.get_barrier_semaphore(), self.px + self.py - 2)


def remote(src, dst, send, recv, device):
    return pltpu.make_async_remote_copy(
        src_ref=src, dst_ref=dst, send_sem=send, recv_sem=recv, device_id=device, device_id_type=MESH,
    )


def remote_kernel(px, py, second_ref, flow_ref, cot_ref, tyf_ref, tyb_ref, core_ref, win_ref, wout_ref,
                  first_ref, third_ref, scale_ref, tzf_ref, txf_ref, tzb_ref, txb_ref,
                  real_h_out, real_l_out, core_out, pack_out,
                  tile, kron, lines_h, lines_l, modes_h, modes_l, tyf, tyb, core, summed, from_mate, to_cross,
                  from_cross, to_row, gathered, lifted, backed, mixed, core_rows, kernel_rows, grads, back_row,
                  blocks, back_h, back_l, real_h, real_l, totals, partial, ranks_in, ranks_sum, ranks_col,
                  core_all, pack_sum, pack_row, pack_col,
                  load_sem, table_sem, mate_send, mate_recv, cross_send, cross_recv, row_send, row_recv,
                  brow_send, brow_recv, bcross_send, bcross_recv, bmate_send, bmate_recv, real_sem,
                  rs_send, rs_recv, cs_send, cs_recv, ag_send, ag_recv, bg_send, bg_recv,
                  pr_send, pr_recv, pc_send, pc_recv):
    here = Place(px, py)
    p, q = here.p, here.q
    k = q * px + p
    steps, channels, group, cols, depth = tile.shape
    tiles = steps // 2
    ranks = win_ref.shape[0]
    packs = ranks // 4
    r1, m1 = first_ref.shape
    r3, m3 = third_ref.shape
    r2 = second_ref.shape[0]
    wide = packs * LANES

    here.greet()
    for t in range(steps):
        source = flow_ref if t < tiles else cot_ref
        pltpu.make_async_copy(
            source.at[:, pl.ds((t % tiles) * group, group)], tile.at[t], load_sem.at[t]).start()
    tables = [pltpu.make_async_copy(tyf_ref.at[q], tyf, table_sem.at[0]),
              pltpu.make_async_copy(tyb_ref.at[q], tyb, table_sem.at[1]),
              pltpu.make_async_copy(core_ref, core, table_sem.at[2])]
    for copy in tables:
        copy.start()
    for f, weight in enumerate((win_ref, wout_ref)):
        high, low = spread(weight[...], NN)
        kron[f, :ranks * SUB] = high
        kron[f, ranks * SUB:] = low
    totals[...] = jnp.zeros_like(totals)
    tables[0].wait()

    def mate_copies(t):
        return [remote(summed.at[t, 2 * s + 1 - here.core], from_mate.at[t, s],
                       mate_send.at[t, s], mate_recv.at[t, s], here.mate) for s in range(2)]

    def cross_copy(t):
        return remote(to_cross.at[t], from_cross.at[t], cross_send.at[t], cross_recv.at[t], here.cross)

    def row_copy(t, step):
        return remote(to_row.at[t, here.row_peer(step)], gathered.at[t // tiles, p, lax.rem(t, tiles)],
                      row_send.at[t, step], row_recv.at[t, step], {"px": here.row_peer(step)})

    def compute(t):
        f = t // tiles

        def lift(x, carry):
            sides = [tile[t, :, x, h * SUB:(h + 1) * SUB, :].reshape(channels * SUB, depth)
                     for h in range(cols // SUB)]
            both = mul(kron[f], jnp.concatenate(sides, axis=1))
            high, low = halves(both[:ranks * SUB] + both[ranks * SUB:])
            for a in range(ranks):
                for h in range(cols // SUB):
                    row = pl.multiple_of(x * (packs * cols) + (a // 4) * cols + h * SUB, SUB)
                    spot = (pl.ds(row, SUB), slice((a % 4) * depth, (a % 4 + 1) * depth))
                    part = (slice(a * SUB, (a + 1) * SUB), slice(h * depth, (h + 1) * depth))
                    lines_h[spot] = high[part]
                    lines_l[spot] = low[part]
            return carry

        lax.fori_loop(0, group, lift, 0)
        modes = mul3((lines_h[...], lines_l[...]), (tzf_ref[0], tzf_ref[1]))
        high, low = halves(modes)
        for x in range(group):
            for a in range(packs):
                for o in range(2):
                    spot = (slice((x * 2 + o) * cols, (x * 2 + o + 1) * cols), slice(a * LANES, (a + 1) * LANES))
                    part = (slice((x * packs + a) * cols, (x * packs + a + 1) * cols),
                            slice(o * LANES, (o + 1) * LANES))
                    modes_h[spot] = high[part]
                    modes_l[spot] = low[part]
        total = mul3((tyf[0], tyf[1]), (modes_h[...], modes_l[...]))
        summed[t] = total.reshape(summed.shape[1:])

    def kernel_side():
        tables[2].wait()

        def one(a, carry):
            for r in range(r1):
                total = second_ref[0, k] * core[a, r, 0]
                for s in range(1, r2):
                    total = total + second_ref[s, k] * core[a, r, s]
                core_rows[pl.ds(pl.multiple_of((a * r1 + r) * r3, r3), r3), :ranks] = total
            return carry

        core_rows[...] = jnp.zeros_like(core_rows)
        lax.fori_loop(0, ranks, one, 0)
        kernel_rows[...] = exact(folded(), widen())

    def folded():
        total = core_rows[pl.ds(0, ranks * r1, stride=r3), :]
        for t in range(1, r3):
            total = total + pltpu.roll(core_rows[pl.ds(t, ranks * r1, stride=r3), :], (r3 - t) * ranks, 1)
        return total

    def widen():
        tall = one_hot(LANES, r3, lambda r: (r3 - r // ranks) % r3, lambda c: c).astype(F32)
        flat = one_hot(m3, wide, lambda r: r, lambda c: c % m3).astype(F32)
        full = exact(exact(tall, third_ref[...]), flat)
        return jnp.where(one_hot(LANES, wide, lambda r: r % ranks, lambda c: c // m3), full, 0.0)

    def body(t, carry):
        @pl.when(t < steps)
        def _():
            pltpu.make_async_copy(flow_ref.at[:, pl.ds(0, group)], tile.at[t], load_sem.at[t]).wait()
            compute(t)

        @pl.when(t == 0)
        def _():
            here.meet()

        @pl.when(t < steps)
        def _():
            for copy in mate_copies(t):
                copy.start()

        @pl.when((t >= 1) & (t < steps + 1))
        def _():
            u = t - 1
            for copy in mate_copies(u):
                copy.wait_recv()
            to_cross[u] = summed[u, 2 * (1 - here.side) + here.core] + from_mate[u, 1 - here.side]
            cross_copy(u).start()

        @pl.when(t == steps)
        def _():
            kernel_side()

        @pl.when(t >= 3)
        def _():
            u = t - 3
            cross_copy(u).wait_recv()
            to_row[u] = summed[u, 2 * here.side + here.core] + from_mate[u, here.side] + from_cross[u]
            for step in range(1, px):
                row_copy(u, step).start()
            gathered[u // tiles, p, lax.rem(u, tiles)] = to_row[u, p]

        return carry

    lax.fori_loop(0, steps + 3, body, 0)
    scale = scale_ref[...]
    for f in range(2):
        for t in range(f * tiles, (f + 1) * tiles):
            for step in range(1, px):
                row_copy(t, step).wait_recv()
        lines = mul3((txf_ref[0], txf_ref[1]), halves(gathered[f].reshape(-1, wide)))
        for o in range(2):
            for a in range(packs):
                cell = lines[o * m1:(o + 1) * m1, a * LANES:(a + 1) * LANES]
                if f == 0:
                    lifted[o, a] = cell
                else:
                    backed[o, a] = cell * scale

    group_of = iota((m1, LANES), 1) // m3
    lay = one_hot(r1 * LANES, r1, lambda r: r // LANES, lambda c: c).astype(F32)
    columns = exact(first_ref[...], lay, (((0,), (1,)), ((), ())))
    mixed[...] = jnp.zeros_like(mixed)

    def around(v):
        v = v + pltpu.roll(v, 64, 1)
        return v + pltpu.roll(v, 32, 1)

    def blend(a, carry):
        mine = group_of == lax.rem(a, 4)
        block = kernel_rows[pl.ds(pl.multiple_of(a * r1, r1), r1), :]
        kern = []
        for b in range(packs):
            total = columns[:, :LANES] * block[0:1, b * LANES:(b + 1) * LANES]
            for r in range(1, r1):
                total = total + columns[:, r * LANES:(r + 1) * LANES] * block[r:r + 1, b * LANES:(b + 1) * LANES]
            kern.append(total)
        grad = [None] * packs
        for o in range(2):
            lift = around(jnp.where(mine, lifted[o, a // 4], 0.0))
            sums = None
            for b in range(packs):
                back = backed[o, b]
                term = kern[b] * back
                sums = term if sums is None else sums + term
                mixed[1, o, b] += kern[b] * lift
                term = lift * back
                grad[b] = term if o == 0 else grad[b] + term
            mixed[0, o, a // 4] += jnp.where(mine, around(sums), 0.0)
        for b in range(packs):
            grads[:, pl.ds(pl.multiple_of((a * packs + b) * LANES, LANES), LANES)] = grad[b]
        return carry

    lax.fori_loop(0, ranks, blend, 0)

    def brow_copy(t, step):
        to = here.row_peer(step)
        return remote(back_row.at[t // tiles, to, lax.rem(t, tiles)], blocks.at[t, q, p],
                      brow_send.at[t, step], brow_recv.at[t, step], {"px": to})

    def bcross_copy(t):
        return remote(blocks.at[t, q], blocks.at[t, q], bcross_send.at[t], bcross_recv.at[t], here.cross)

    def bmate_copy(t, s):
        quarter = q if s == 0 else lax.rem(q + 2, py)
        return remote(blocks.at[t, quarter], blocks.at[t, quarter],
                      bmate_send.at[t, s], bmate_recv.at[t, s], here.mate)

    share = partial.shape[0] // px

    def rs_copy(step):
        to = here.row_peer(step)
        return remote(partial.at[pl.ds(to * share, share)], ranks_in.at[p], rs_send.at[step], rs_recv.at[step],
                      {"px": to})

    def cs_copy(step):
        to = here.col_peer(step)
        return remote(ranks_sum.at[to], ranks_col.at[q], cs_send.at[step], cs_recv.at[step], {"py": to})

    def ag_copy(step):
        return remote(core_all.at[p, q], core_all.at[p, q], ag_send.at[step], ag_recv.at[step],
                      {"px": here.row_peer(step)})

    def bg_copy(s):
        quarter = lax.rem(q + 2, py) if s == 2 else q
        return remote(core_all.at[:, quarter], core_all.at[:, quarter], bg_send.at[s], bg_recv.at[s],
                      here.cross if s == 0 else here.mate)

    def pr_copy(step):
        return remote(pack_sum.at[0], pack_row.at[p], pr_send.at[step], pr_recv.at[step],
                      {"px": here.row_peer(step)})

    def pc_copy(step):
        return remote(pack_sum.at[1], pack_col.at[q], pc_send.at[step], pc_recv.at[step],
                      {"py": here.col_peer(step)})

    def rows_out(f):
        pieces = [jnp.concatenate([mixed[f, o, b] for b in range(packs)], axis=1) for o in range(2)]
        lines = jnp.concatenate(pieces, axis=0)
        if f == 1:
            lines = lines * jnp.concatenate([scale] * packs, axis=1)
        back_row[f] = mul3((txb_ref[0], txb_ref[1]), halves(lines)).reshape(back_row.shape[1:])
        for t in range(f * tiles, (f + 1) * tiles):
            for step in range(1, px):
                brow_copy(t, step).start()
            blocks[t, q, p] = back_row[f, p, t - f * tiles]

    rows_out(0)
    whole = grads[...]
    thin = exact(first_ref[...], whole)
    tall = jnp.concatenate([thin[:, a * wide:(a + 1) * wide] for a in range(ranks)], axis=0)
    broad = widen()
    part = exact(tall, broad, NT)
    partial[...] = part
    for step in range(1, px):
        rs_copy(step).start()
    ranks_in[p] = partial[pl.ds(pl.multiple_of(p * share, share), share), :]
    rows_out(1)
    tables[1].wait()

    spread_rows = jnp.concatenate([kernel_rows[a * r1:(a + 1) * r1, :] for a in range(ranks)], axis=1)
    grad_first = exact(spread_rows, whole, NT)
    cross = exact(folded(), tall, TN)
    cross = jnp.where(one_hot(LANES, wide, lambda r: r % ranks, lambda c: c // m3), cross, 0.0)
    cross = cross.reshape(r3, ranks, wide).sum(axis=1)
    cross = exact(one_hot(r3, r3, lambda r: (r3 - r) % r3, lambda c: c).astype(F32), cross)
    grad_third = exact(cross, one_hot(wide, m3, lambda r: r % m3, lambda c: c).astype(F32))
    lane = iota((r1, LANES), 1)
    row = iota((r1, LANES), 0)
    small = exact(grad_first, one_hot(m1, LANES, lambda r: r, lambda c: c).astype(F32))
    small = small + exact(grad_third, one_hot(m3, LANES, lambda r: r + m1, lambda c: c).astype(F32))

    def second(a, sums):
        rows = partial[pl.ds(pl.multiple_of(a * r1, r1), r1), :]
        sums = list(sums)
        for r in range(r1):
            cell = unfold(rows[r:r + 1], r3, ranks)[:, :ranks]
            for s in range(r2):
                sums[s] = sums[s] + core[a, r, s] * cell
        return tuple(sums)

    sums = lax.fori_loop(0, ranks, second, tuple(jnp.zeros((r3, ranks), F32) for _ in range(r2)))
    for s in range(r2):
        small = small + jnp.where((lane == k + m1 + m3) & (row == s), jnp.sum(sums[s]), 0.0)
    pack_sum[0, ranks:ranks + r1] = small

    def slot(t):
        return jnp.maximum(t - tiles + 1, 0)

    def place(t):
        here_slot = slot(t)
        high, low = halves(blocks[t].reshape(-1, wide))
        modes = mul3((tyb[0], tyb[1]), (high, low))
        high, low = halves(modes)
        for x in range(group):
            for a in range(packs):
                for o in range(2):
                    part = (slice((x * 2 + o) * cols, (x * 2 + o + 1) * cols), slice(a * LANES, (a + 1) * LANES))
                    spot = (slice((x * packs + a) * cols, (x * packs + a + 1) * cols),
                            slice(o * LANES, (o + 1) * LANES))
                    back_h[spot] = high[part]
                    back_l[spot] = low[part]
        real = mul3((back_h[...], back_l[...]), (tzb_ref[0], tzb_ref[1]))
        high, low = halves(real)
        for x in range(group):
            for a in range(ranks):
                for h in range(cols // SUB):
                    row = (x * packs + a // 4) * cols + h * SUB
                    part = (slice(row, row + SUB), slice((a % 4) * depth, (a % 4 + 1) * depth))
                    spot = (here_slot, x, slice(a * SUB, (a + 1) * SUB), slice(h * depth, (h + 1) * depth))
                    real_h[spot] = high[part]
                    real_l[spot] = low[part]

    def outer(t):
        def one(x, carry):
            sides = [tile[t, :, x, h * SUB:(h + 1) * SUB, :].reshape(channels * SUB, depth)
                     for h in range(cols // SUB)]
            cells = jnp.concatenate(sides, axis=1)
            totals[t // tiles] += mul(cells, real_h[slot(t), x], NT) + mul(cells, real_l[slot(t), x], NT)
            return carry

        lax.fori_loop(0, group, one, 0)

    def real_copies(t):
        u = t - tiles
        return [pltpu.make_async_copy(real_h.at[u + 1], real_h_out.at[u], real_sem.at[u, 0]),
                pltpu.make_async_copy(real_l.at[u + 1], real_l_out.at[u], real_sem.at[u, 1])]

    def back_body(i, carry):
        @pl.when(i < steps)
        def _():
            for step in range(1, px):
                brow_copy(i, step).wait_recv()
            bcross_copy(i).start()
            bmate_copy(i, 0).start()

        @pl.when((i >= 2) & (i < steps + 2))
        def _():
            bcross_copy(i - 2).wait_recv()
            bmate_copy(i - 2, 1).start()

        @pl.when(i >= 3)
        def _():
            t = i - 3
            for s in range(2):
                bmate_copy(t, s).wait_recv()
            place(t)
            outer(t)

        @pl.when(i >= 3 + tiles)
        def _():
            for copy in real_copies(i - 3):
                copy.start()

        @pl.when(i == 5)
        def _():
            for step in range(1, px):
                rs_copy(step).wait_recv()
            for s in range(r2):
                total = None
                for o in range(px):
                    term = ranks_in[o] * second_ref[s, q * px + o]
                    total = term if total is None else total + term
                ranks_sum[s // 2, s % 2] = total
            ranks_col[q] = ranks_sum[q]
            for step in range(1, py):
                cs_copy(step).start()

        @pl.when(i == 6)
        def _():
            for step in range(1, py):
                cs_copy(step).wait_recv()
            total = ranks_col[0]
            for s in range(1, py):
                total = total + ranks_col[s]
            core_all[p, q] = total
            for step in range(1, px):
                ag_copy(step).start()

        @pl.when(i == 8)
        def _():
            for step in range(1, px):
                ag_copy(step).wait_recv()
            bg_copy(0).start()
            bg_copy(1).start()

        return carry

    lax.fori_loop(0, steps + 3, back_body, 0)
    bg_copy(0).wait_recv()
    bg_copy(2).start()
    keep = one_hot(channels * SUB, ranks * SUB, lambda r: r % SUB, lambda c: c % SUB)
    grids = [jnp.where(keep, totals[f], 0.0).reshape(channels, SUB, ranks * SUB).sum(axis=1) for f in range(2)]
    pick = one_hot(ranks, ranks * SUB, lambda r: r, lambda c: c // SUB).astype(F32)
    pack_sum[0, :ranks] = exact(pick, jnp.concatenate(grids, axis=0), NT)
    for step in range(1, px):
        pr_copy(step).start()
    pack_row[p] = pack_sum[0]
    bg_copy(1).wait_recv()
    bg_copy(2).wait_recv()
    core_out[...] = core_all[...]
    for step in range(1, px):
        pr_copy(step).wait_recv()
    total = pack_row[0]
    for s in range(1, px):
        total = total + pack_row[s]
    pack_sum[1] = total
    for step in range(1, py):
        pc_copy(step).start()
    pack_col[q] = total

    def drain(t, carry):
        for copy in mate_copies(t):
            copy.wait_send()
        cross_copy(t).wait_send()
        bcross_copy(t).wait_send()
        for s in range(2):
            bmate_copy(t, s).wait_send()
        for step in range(1, px):
            row_copy(t, step).wait_send()
            brow_copy(t, step).wait_send()
        return carry

    lax.fori_loop(0, steps, drain, 0)
    for step in range(1, px):
        for copy in (rs_copy, ag_copy, pr_copy):
            copy(step).wait_send()
    for s in range(3):
        bg_copy(s).wait_send()
    for t in range(tiles, steps):
        for copy in real_copies(t):
            copy.wait()
    for step in range(1, py):
        cs_copy(step).wait_send()
        pc_copy(step).wait_recv()
    total = pack_col[0]
    for s in range(1, py):
        total = total + pack_col[s]
    pack_out[...] = total
    for step in range(1, py):
        pc_copy(step).wait_send()


def emit_kernel(high_ref, low_ref, core_ref, pack_ref, wout_ref, out_ref, core_out, in_out, oo_out,
                first_out, second_out, third_out, kron):
    ranks, channels = wout_ref.shape
    cols, depth = out_ref.shape[2:]
    _, r1, r2, r3, _ = core_out.shape
    m1, m3 = first_out.shape[1], third_out.shape[1]
    m2 = second_out.shape[1]

    @pl.when(pl.program_id(0) == 0)
    def _():
        kron[0], kron[1] = spread(wout_ref[...], NT)
        in_out[...] = pack_ref[:ranks, :channels]
        oo_out[...] = pack_ref[:ranks, channels:2 * channels]
        first_out[...] = pack_ref[ranks:ranks + r1, :m1]
        third_out[...] = pack_ref[ranks:ranks + r1, m1:m1 + m3]
        second_out[...] = pack_ref[ranks:ranks + r1, m1 + m3:m1 + m3 + m2]

    def one(x, carry):
        both = mul3((kron[0], kron[1]), (high_ref[0, x], low_ref[0, x])).astype(BF16)
        for h in range(cols // SUB):
            out_ref[:, x, h * SUB:(h + 1) * SUB, :] = both[:, h * depth:(h + 1) * depth].reshape(
                channels, SUB, depth)
        return carry

    lax.fori_loop(0, out_ref.shape[1], one, 0)
    per = core_ref.shape[2]

    def two(a, carry):
        for s in range(r2):
            rows = core_ref[0, s // per, s % per, pl.ds(pl.multiple_of(a * r1, r1), r1), :]
            for r in range(r1):
                core_out[a, r, s] = unfold(rows[r:r + 1], r3, ranks)[:, :ranks]
        return carry

    lax.fori_loop(0, core_out.shape[0], two, 0)


def fast_shards(px, py, flow_field, cotangent, tucker_core, in_factor, out_factor,
                first_factor, second_factor, third_factor):
    channels, rows, cols, depth = flow_field.shape
    ri, ro, r1, r2, r3 = tucker_core.shape
    group = 2 * LANES // (2 * cols)
    tiles = rows // group
    steps = 2 * tiles
    packs = ri // 4
    wide = packs * LANES
    keep = px
    inverse_count = 1.0 / (NX * NY * NZ)

    small = np_depth(NZ, M3)
    tz = np.einsum("st,pzm->szptm", np.eye(4), small).reshape(4 * depth, 2 * 4 * M3)
    turn = np_turn(M2, NY).reshape(2, py, cols, 2, py, keep)
    ty = np.einsum("pdyoqk,xw->dqkxowpy", turn, np.eye(group))
    ty = ty.reshape(py, py * keep * group * 2, group * 2 * cols)
    turn = np_turn(M1, NX).reshape(2, NX, 2, M1)
    tx = turn.transpose(2, 3, 1, 0).reshape(2 * M1, NX * 2)
    tz_f, tz_b = np_halves(tz), np_halves(tz.T)
    ty_f = np_halves(ty).swapaxes(0, 1)
    ty_b = np_halves(ty.swapaxes(1, 2)).swapaxes(0, 1)
    tx_f, tx_b = np_halves(tx), np_halves(tx.T)
    weight = np.where(np.arange(M3) == 0, 1.0, 2.0) * inverse_count
    scale = jnp.asarray(np.tile(weight, 4)[None, :].astype(np.float32))

    vmem = pl.BlockSpec(memory_space=pltpu.VMEM)
    smem = pl.BlockSpec(memory_space=pltpu.SMEM)
    anywhere = pl.BlockSpec(memory_space=pl.ANY)
    shape = jax.ShapeDtypeStruct
    dma = pltpu.SemaphoreType.DMA

    def buf(*dims):
        return pltpu.VMEM(dims, F32)

    def thin(*dims):
        return pltpu.VMEM(dims, BF16)

    lines = group * packs * cols
    block = (keep, 2 * group, wide)
    real = (group, ri * SUB, cols // SUB * depth)
    count = ri * r1
    spectrum = (2, packs, M1, LANES)
    piece = (r2 // py, count // px, LANES)
    pack = (ri + r1, LANES)
    core = tucker_core.transpose(0, 2, 3, 4, 1)
    high, low, core_sum, packed = pl.pallas_call(
        functools.partial(remote_kernel, px, py),
        out_shape=(shape((tiles,) + real, BF16), shape((tiles,) + real, BF16),
                   shape((px, py) + piece, F32), shape(pack, F32)),
        in_specs=[smem] + [anywhere] * 5 + [vmem] * 9,
        out_specs=(anywhere, anywhere, vmem, vmem),
        scratch_shapes=[
            thin(steps, channels, group, cols, depth),
            thin(2, 2 * ri * SUB, channels * SUB),
            thin(lines, 4 * depth), thin(lines, 4 * depth),
            thin(group * 2 * cols, wide), thin(group * 2 * cols, wide),
            thin(*ty_f.shape[1:]), thin(*ty_b.shape[1:]), buf(*core.shape),
            buf(steps, py, *block), buf(steps, 2, *block), buf(steps, *block), buf(steps, *block),
            buf(steps, *block), buf(2, px, tiles, 2 * group, wide),
            buf(*spectrum), buf(*spectrum), buf(2, *spectrum),
            buf(count * r3, LANES), buf(count, wide), buf(M1, ri * wide),
            buf(2, px, tiles, 2 * group, wide), buf(steps, py, *block),
            thin(lines, 2 * LANES), thin(lines, 2 * LANES), thin(tiles + 1, *real), thin(tiles + 1, *real),
            buf(2, channels * SUB, ri * SUB),
            buf(count, LANES), buf(px, count // px, LANES), buf(py, *piece), buf(py, *piece),
            buf(px, py, *piece), buf(2, *pack), buf(px, *pack), buf(py, *pack),
            dma((steps,)), dma((3,)),
            dma((steps, 2)), dma((steps, 2)), dma((steps,)), dma((steps,)), dma((steps, px)), dma((steps, px)),
            dma((steps, px)), dma((steps, px)), dma((steps,)), dma((steps,)), dma((steps, 2)), dma((steps, 2)),
            dma((tiles, 2)),
            dma((px,)), dma((px,)), dma((py,)), dma((py,)), dma((px,)), dma((px,)), dma((3,)), dma((3,)),
            dma((px,)), dma((px,)), dma((py,)), dma((py,)),
        ],
        compiler_params=pltpu.CompilerParams(
            vmem_limit_bytes=VMEM_LIMIT, collective_id=0, has_side_effects=True),
    )(second_factor.T, flow_field, cotangent, jnp.asarray(ty_f), jnp.asarray(ty_b), core, in_factor.T,
      out_factor.T, first_factor.T, third_factor.T, scale,
      jnp.asarray(tz_f), jnp.asarray(tx_f), jnp.asarray(tz_b), jnp.asarray(tx_b))

    span = rows // px
    whole = lambda *dims: pl.BlockSpec(dims, lambda i: (0,) * len(dims))
    out, core_grad, in_grad, out_grad, first_grad, second_grad, third_grad = pl.pallas_call(
        emit_kernel, grid=(px,),
        out_shape=(
            shape(flow_field.shape, BF16), shape(core.shape, F32), shape((ri, channels), F32),
            shape((ro, channels), F32), shape((r1, M1), F32), shape((r2, M2), F32), shape((r3, M3), F32),
        ),
        in_specs=[
            pl.BlockSpec((1, span) + real[1:], lambda i: (i * span // group, i % (group // span), 0, 0)),
            pl.BlockSpec((1, span) + real[1:], lambda i: (i * span // group, i % (group // span), 0, 0)),
            pl.BlockSpec((1,) + (py,) + piece, lambda i: (i, 0, 0, 0, 0)),
            whole(*pack), whole(ro, channels),
        ],
        out_specs=(
            pl.BlockSpec((channels, span, cols, depth), lambda i: (0, i, 0, 0)),
            pl.BlockSpec((ri // px, r1, r2, r3, ro), lambda i: (i, 0, 0, 0, 0)),
            whole(ri, channels), whole(ro, channels), whole(r1, M1), whole(r2, M2), whole(r3, M3),
        ),
        scratch_shapes=[thin(2, channels * SUB, ro * SUB)],
        compiler_params=pltpu.CompilerParams(vmem_limit_bytes=VMEM_LIMIT),
    )(high, low, core_sum, packed, out_factor.T)
    return (out, core_grad.transpose(0, 4, 1, 2, 3), in_grad.T, out_grad.T, first_grad.T, second_grad.T,
            third_grad.T)


def solution(mesh):
    px, py = mesh.shape["px"], mesh.shape["py"]
    rows, cols = NX // px, NY // py
    fits = py == 4 and px * py == M2 and cols == 32 and rows == 16 and NZ == LANES
    fits = fits and M1 == 32 and M3 == 32
    body = functools.partial(fast_shards, px, py) if fits else shards
    return jax.shard_map(
        body,
        mesh=mesh,
        in_specs=(
            P(None, "px", "py", None),
            P(None, "px", "py", None),
            P(),
            P(),
            P(),
            P(),
            P(),
            P(),
        ),
        out_specs=(P(None, "px", "py", None), P(), P(), P(), P(), P(), P()),
        check_vma=False,
    )
```

time: 200 us -> 125 us (0.62)
  local copies, waits for them, and re-layouts: 62.6 us -> 0 us
  Pallas kernels: 136 us -> 124 us
    reshape x5 -> x0, local copies, waits for them, and re-layouts: 34.2 us -> none  [the longest x2 13.5 us: fast_shards(): core = core.reshape(r2, ro * packs * r1, 4 * r3)]
    unnamed x19 -> x0, local copies, waits for them, and re-layouts: 16.9 us -> none
    pallas_call x3 -> x2, Pallas kernels: 136 us -> 124 us  [the longest x1 110 us: fast_shards(): pl.pallas_call(functools.partial(remote_kernel, px, py), out_shape=(shape...]
    transpose x1 -> x0, local copies, waits for them, and re-layouts: 9.04 us -> none  [fast_shards(): core_sum.reshape(ro, packs, r1, r2, 4, r3).transpose(1, 4, 0, 2, 3, 5)]
where the time goes in v1:
time: 125 us
  Pallas kernels  124 us (99%)
    pallas_call x1, Pallas kernels, fast_shards(): pl.pallas_call(functools.partial(remote_kernel, px, py), out_shape=(shape...  110 us
    pallas_call x1, Pallas kernels, fast_shards(): pl.pallas_call(emit_kernel, grid=(px,), out_shape=(shape(flow_field.shape...  14.7 us

profile of v1, /device:TPU:0, one launch (start us, length us, event | category | flops | bytes accessed | tf_op | source)
XLA Modules:
  0.0 125.0 jit_solution(890145461218471506)
XLA Ops:
  0.6 109.7 %shard_map.198 = (bf16[4,4,256,256]{3,2,1,0:T(8,128)(2,1)}, bf16[4,4,256,256]{3,2,1,0:T(8,128)(2,1)}, f32[8,4,2,16,128]{4,3,2,1,0:T(8,128)}, f32[24,128]{1,0:T(8,128)}) custom-call(f32[8,32]{1,0:T(8,128)} %bitcast.16, bf16[64,16,32,128]{3,2,1,0:T(8,128)(2,1)} %flow_ref.1, bf16[64,16,32,128]{3,2,1,0:T(8,128)(2,1)} %cot_ref.1, ...), custom_call_target="tpu_custom_call" | custom-call | tf_op jit(solution)/shard_map/pallas_call | solution.py:783
  110.3 14.7 %shard_map.199 = (bf16[64,16,32,128]{3,2,1,0:T(8,128)(2,1)}, f32[16,8,8,8,16]{4,3,2,1,0:T(8,128)}, f32[16,64]{1,0:T(8,128)}, f32[16,64]{1,0:T(8,128)}, f32[8,32]...) custom-call(bf16[4,4,256,256]{3,2,1,0:T(8,128)(2,1)} %get-tuple-element.18.high_ref, ...), custom_call_target="tpu_custom_call" | custom-call | tf_op jit(solution)/shard_map/pallas_call | solution.py:819

commit v2 on v1

--- a/solution.py
+++ b/solution.py
@@ -253,13 +253,13 @@
 
 def remote_kernel(px, py, second_ref, flow_ref, cot_ref, tyf_ref, tyb_ref, core_ref, win_ref, wout_ref,
                   first_ref, third_ref, scale_ref, tzf_ref, txf_ref, tzb_ref, txb_ref,
-                  real_h_out, real_l_out, core_out, pack_out,
+                  out_ref, core_out, pack_out,
                   tile, kron, lines_h, lines_l, modes_h, modes_l, tyf, tyb, core, summed, from_mate, to_cross,
                   from_cross, to_row, gathered, lifted, backed, mixed, core_rows, kernel_rows, grads, back_row,
-                  blocks, back_h, back_l, real_h, real_l, totals, partial, ranks_in, ranks_sum, ranks_col,
+                  blocks, krono, real_h, real_l, totals, partial, ranks_in, ranks_sum, ranks_col,
                   core_all, pack_sum, pack_row, pack_col,
                   load_sem, table_sem, mate_send, mate_recv, cross_send, cross_recv, row_send, row_recv,
-                  brow_send, brow_recv, bcross_send, bcross_recv, bmate_send, bmate_recv, real_sem,
+                  brow_send, brow_recv, bcross_send, bcross_recv, bmate_send, bmate_recv, out_sem,
                   rs_send, rs_recv, cs_send, cs_recv, ag_send, ag_recv, bg_send, bg_recv,
                   pr_send, pr_recv, pc_send, pc_recv):
     here = Place(px, py)
@@ -282,7 +282,7 @@
     tables = [pltpu.make_async_copy(tyf_ref.at[q], tyf, table_sem.at[0]),
               pltpu.make_async_copy(tyb_ref.at[q], tyb, table_sem.at[1]),
               pltpu.make_async_copy(core_ref, core, table_sem.at[2])]
-    for copy in tables:
+    for copy in tables[:2]:
         copy.start()
     for f, weight in enumerate((win_ref, wout_ref)):
         high, low = spread(weight[...], NN)
@@ -369,6 +369,7 @@
         @pl.when(t == 0)
         def _():
             here.meet()
+            tables[2].start()
 
         @pl.when(t < steps)
         def _():
@@ -400,7 +401,8 @@
 
     lax.fori_loop(0, steps + 3, body, 0)
     scale = scale_ref[...]
-    for f in range(2):
+
+    def arrive(f):
         for t in range(f * tiles, (f + 1) * tiles):
             for step in range(1, px):
                 row_copy(t, step).wait_recv()
@@ -422,32 +424,39 @@
         v = v + pltpu.roll(v, 64, 1)
         return v + pltpu.roll(v, 32, 1)
 
+    def spots(a):
+        return [pl.ds(pl.multiple_of((a * packs + b) * LANES, LANES), LANES) for b in range(packs)]
+
     def blend(a, carry):
         mine = group_of == lax.rem(a, 4)
         block = kernel_rows[pl.ds(pl.multiple_of(a * r1, r1), r1), :]
-        kern = []
-        for b in range(packs):
+        lift = [around(jnp.where(mine, lifted[o, a // 4], 0.0)) for o in range(2)]
+        for b, lanes in enumerate(spots(a)):
             total = columns[:, :LANES] * block[0:1, b * LANES:(b + 1) * LANES]
             for r in range(1, r1):
                 total = total + columns[:, r * LANES:(r + 1) * LANES] * block[r:r + 1, b * LANES:(b + 1) * LANES]
-            kern.append(total)
-        grad = [None] * packs
+            grads[:, lanes] = total
+            for o in range(2):
+                mixed[0, o, b] += total * lift[o]
+        return carry
+
+    def unblend(a, carry):
+        mine = group_of == lax.rem(a, 4)
+        lift = [around(jnp.where(mine, lifted[o, a // 4], 0.0)) for o in range(2)]
+        sums = [None, None]
+        for b, lanes in enumerate(spots(a)):
+            total = grads[:, lanes]
+            grad = None
+            for o in range(2):
+                back = backed[o, b]
+                term = total * back
+                sums[o] = term if sums[o] is None else sums[o] + term
+                term = lift[o] * back
+                grad = term if grad is None else grad + term
+            grads[:, lanes] = grad
         for o in range(2):
-            lift = around(jnp.where(mine, lifted[o, a // 4], 0.0))
-            sums = None
-            for b in range(packs):
-                back = backed[o, b]
-                term = kern[b] * back
-                sums = term if sums is None else sums + term
-                mixed[1, o, b] += kern[b] * lift
-                term = lift * back
-                grad[b] = term if o == 0 else grad[b] + term
-            mixed[0, o, a // 4] += jnp.where(mine, around(sums), 0.0)
-        for b in range(packs):
-            grads[:, pl.ds(pl.multiple_of((a * packs + b) * LANES, LANES), LANES)] = grad[b]
+            mixed[1, o, a // 4] += jnp.where(mine, around(sums[o]), 0.0)
         return carry
-
-    lax.fori_loop(0, ranks, blend, 0)
 
     def brow_copy(t, step):
         to = here.row_peer(step)
@@ -493,7 +502,7 @@
     def rows_out(f):
         pieces = [jnp.concatenate([mixed[f, o, b] for b in range(packs)], axis=1) for o in range(2)]
         lines = jnp.concatenate(pieces, axis=0)
-        if f == 1:
+        if f == 0:
             lines = lines * jnp.concatenate([scale] * packs, axis=1)
         back_row[f] = mul3((txb_ref[0], txb_ref[1]), halves(lines)).reshape(back_row.shape[1:])
         for t in range(f * tiles, (f + 1) * tiles):
@@ -501,47 +510,56 @@
                 brow_copy(t, step).start()
             blocks[t, q, p] = back_row[f, p, t - f * tiles]
 
+    arrive(0)
+    lax.fori_loop(0, ranks, blend, 0)
     rows_out(0)
-    whole = grads[...]
-    thin = exact(first_ref[...], whole)
-    tall = jnp.concatenate([thin[:, a * wide:(a + 1) * wide] for a in range(ranks)], axis=0)
-    broad = widen()
-    part = exact(tall, broad, NT)
-    partial[...] = part
-    for step in range(1, px):
-        rs_copy(step).start()
-    ranks_in[p] = partial[pl.ds(pl.multiple_of(p * share, share), share), :]
+    arrive(1)
+    lax.fori_loop(0, ranks, unblend, 0)
     rows_out(1)
     tables[1].wait()
-
-    spread_rows = jnp.concatenate([kernel_rows[a * r1:(a + 1) * r1, :] for a in range(ranks)], axis=1)
-    grad_first = exact(spread_rows, whole, NT)
-    cross = exact(folded(), tall, TN)
-    cross = jnp.where(one_hot(LANES, wide, lambda r: r % ranks, lambda c: c // m3), cross, 0.0)
-    cross = cross.reshape(r3, ranks, wide).sum(axis=1)
-    cross = exact(one_hot(r3, r3, lambda r: (r3 - r) % r3, lambda c: c).astype(F32), cross)
-    grad_third = exact(cross, one_hot(wide, m3, lambda r: r % m3, lambda c: c).astype(F32))
-    lane = iota((r1, LANES), 1)
-    row = iota((r1, LANES), 0)
-    small = exact(grad_first, one_hot(m1, LANES, lambda r: r, lambda c: c).astype(F32))
-    small = small + exact(grad_third, one_hot(m3, LANES, lambda r: r + m1, lambda c: c).astype(F32))
-
-    def second(a, sums):
-        rows = partial[pl.ds(pl.multiple_of(a * r1, r1), r1), :]
-        sums = list(sums)
-        for r in range(r1):
-            cell = unfold(rows[r:r + 1], r3, ranks)[:, :ranks]
-            for s in range(r2):
-                sums[s] = sums[s] + core[a, r, s] * cell
-        return tuple(sums)
-
-    sums = lax.fori_loop(0, ranks, second, tuple(jnp.zeros((r3, ranks), F32) for _ in range(r2)))
-    for s in range(r2):
-        small = small + jnp.where((lane == k + m1 + m3) & (row == s), jnp.sum(sums[s]), 0.0)
-    pack_sum[0, ranks:ranks + r1] = small
+    high, low = spread(wout_ref[...], NT)
+    krono[0] = high
+    krono[1] = low
+
+    def tall_grads():
+        thin = exact(first_ref[...], grads[...])
+        return jnp.concatenate([thin[:, a * wide:(a + 1) * wide] for a in range(ranks)], axis=0)
+
+    def core_side():
+        partial[...] = exact(tall_grads(), widen(), NT)
+        for step in range(1, px):
+            rs_copy(step).start()
+        ranks_in[p] = partial[pl.ds(pl.multiple_of(p * share, share), share), :]
+
+    def small_side():
+        spread_rows = jnp.concatenate([kernel_rows[a * r1:(a + 1) * r1, :] for a in range(ranks)], axis=1)
+        grad_first = exact(spread_rows, grads[...], NT)
+        cross = exact(folded(), tall_grads(), TN)
+        cross = jnp.where(one_hot(LANES, wide, lambda r: r % ranks, lambda c: c // m3), cross, 0.0)
+        cross = cross.reshape(r3, ranks, wide).sum(axis=1)
+        cross = exact(one_hot(r3, r3, lambda r: (r3 - r) % r3, lambda c: c).astype(F32), cross)
+        grad_third = exact(cross, one_hot(wide, m3, lambda r: r % m3, lambda c: c).astype(F32))
+        lane = iota((r1, LANES), 1)
+        row = iota((r1, LANES), 0)
+        small = exact(grad_first, one_hot(m1, LANES, lambda r: r, lambda c: c).astype(F32))
+        small = small + exact(grad_third, one_hot(m3, LANES, lambda r: r + m1, lambda c: c).astype(F32))
+
+        def second(a, sums):
+            rows = partial[pl.ds(pl.multiple_of(a * r1, r1), r1), :]
+            sums = list(sums)
+            for r in range(r1):
+                cell = unfold(rows[r:r + 1], r3, ranks)[:, :ranks]
+                for s in range(r2):
+                    sums[s] = sums[s] + core[a, r, s] * cell
+            return tuple(sums)
+
+        sums = lax.fori_loop(0, ranks, second, tuple(jnp.zeros((r3, ranks), F32) for _ in range(r2)))
+        for s in range(r2):
+            small = small + jnp.where((lane == k + m1 + m3) & (row == s), jnp.sum(sums[s]), 0.0)
+        pack_sum[0, ranks:ranks + r1] = small
 
     def slot(t):
-        return jnp.maximum(t - tiles + 1, 0)
+        return (t + 1) * (1 - t // tiles)
 
     def place(t):
         here_slot = slot(t)
@@ -554,9 +572,10 @@
                     part = (slice((x * 2 + o) * cols, (x * 2 + o + 1) * cols), slice(a * LANES, (a + 1) * LANES))
                     spot = (slice((x * packs + a) * cols, (x * packs + a + 1) * cols),
                             slice(o * LANES, (o + 1) * LANES))
-                    back_h[spot] = high[part]
-                    back_l[spot] = low[part]
-        real = mul3((back_h[...], back_l[...]), (tzb_ref[0], tzb_ref[1]))
+                    lines_h[spot] = high[part]
+                    lines_l[spot] = low[part]
+        half = 2 * LANES
+        real = mul3((lines_h[:, :half], lines_l[:, :half]), (tzb_ref[0], tzb_ref[1]))
         high, low = halves(real)
         for x in range(group):
             for a in range(ranks):
@@ -568,19 +587,30 @@
                     real_l[spot] = low[part]
 
     def outer(t):
+        u = lax.rem(t + tiles, steps)
+
         def one(x, carry):
-            sides = [tile[t, :, x, h * SUB:(h + 1) * SUB, :].reshape(channels * SUB, depth)
+            sides = [tile[u, :, x, h * SUB:(h + 1) * SUB, :].reshape(channels * SUB, depth)
                      for h in range(cols // SUB)]
             cells = jnp.concatenate(sides, axis=1)
-            totals[t // tiles] += mul(cells, real_h[slot(t), x], NT) + mul(cells, real_l[slot(t), x], NT)
+            totals[u // tiles] += mul(cells, real_h[slot(t), x], NT) + mul(cells, real_l[slot(t), x], NT)
             return carry
 
         lax.fori_loop(0, group, one, 0)
 
-    def real_copies(t):
-        u = t - tiles
-        return [pltpu.make_async_copy(real_h.at[u + 1], real_h_out.at[u], real_sem.at[u, 0]),
-                pltpu.make_async_copy(real_l.at[u + 1], real_l_out.at[u], real_sem.at[u, 1])]
+    def out_copy(g):
+        return pltpu.make_async_copy(tile.at[tiles + g], out_ref.at[:, pl.ds(g * group, group)], out_sem.at[g])
+
+    def emit(g):
+        def one(x, carry):
+            both = mul3((krono[0], krono[1]), (real_h[g + 1, x], real_l[g + 1, x])).astype(BF16)
+            for h in range(cols // SUB):
+                tile[tiles + g, :, x, h * SUB:(h + 1) * SUB, :] = both[:, h * depth:(h + 1) * depth].reshape(
+                    channels, SUB, depth)
+            return carry
+
+        lax.fori_loop(0, group, one, 0)
+        out_copy(g).start()
 
     def back_body(i, carry):
         @pl.when(i < steps)
@@ -603,10 +633,17 @@
             place(t)
             outer(t)
 
-        @pl.when(i >= 3 + tiles)
-        def _():
-            for copy in real_copies(i - 3):
-                copy.start()
+        @pl.when((i >= tiles + 1) & (i < tiles + 3))
+        def _():
+            emit(i - tiles - 1)
+
+        @pl.when(i == 2)
+        def _():
+            core_side()
+
+        @pl.when(i == 3)
+        def _():
+            small_side()
 
         @pl.when(i == 5)
         def _():
@@ -622,7 +659,7 @@
             for step in range(1, py):
                 cs_copy(step).start()
 
-        @pl.when(i == 6)
+        @pl.when(i == 7)
         def _():
             for step in range(1, py):
                 cs_copy(step).wait_recv()
@@ -633,7 +670,7 @@
             for step in range(1, px):
                 ag_copy(step).start()
 
-        @pl.when(i == 8)
+        @pl.when(i == 9)
         def _():
             for step in range(1, px):
                 ag_copy(step).wait_recv()
@@ -652,6 +689,7 @@
     for step in range(1, px):
         pr_copy(step).start()
     pack_row[p] = pack_sum[0]
+    emit(tiles - 2)
     bg_copy(1).wait_recv()
     bg_copy(2).wait_recv()
     core_out[...] = core_all[...]
@@ -664,6 +702,7 @@
     for step in range(1, py):
         pc_copy(step).start()
     pack_col[q] = total
+    emit(tiles - 1)
 
     def drain(t, carry):
         for copy in mate_copies(t):
@@ -683,9 +722,6 @@
             copy(step).wait_send()
     for s in range(3):
         bg_copy(s).wait_send()
-    for t in range(tiles, steps):
-        for copy in real_copies(t):
-            copy.wait()
     for step in range(1, py):
         cs_copy(step).wait_send()
         pc_copy(step).wait_recv()
@@ -695,33 +731,26 @@
     pack_out[...] = total
     for step in range(1, py):
         pc_copy(step).wait_send()
-
-
-def emit_kernel(high_ref, low_ref, core_ref, pack_ref, wout_ref, out_ref, core_out, in_out, oo_out,
-                first_out, second_out, third_out, kron):
-    ranks, channels = wout_ref.shape
-    cols, depth = out_ref.shape[2:]
+    for g in range(tiles):
+        out_copy(g).wait()
+
+
+def emit_kernel(field_ref, core_ref, pack_ref, out_ref, core_out, in_out, oo_out,
+                first_out, second_out, third_out):
+    ranks, channels = in_out.shape
     _, r1, r2, r3, _ = core_out.shape
     m1, m3 = first_out.shape[1], third_out.shape[1]
     m2 = second_out.shape[1]
 
     @pl.when(pl.program_id(0) == 0)
     def _():
-        kron[0], kron[1] = spread(wout_ref[...], NT)
         in_out[...] = pack_ref[:ranks, :channels]
         oo_out[...] = pack_ref[:ranks, channels:2 * channels]
         first_out[...] = pack_ref[ranks:ranks + r1, :m1]
         third_out[...] = pack_ref[ranks:ranks + r1, m1:m1 + m3]
         second_out[...] = pack_ref[ranks:ranks + r1, m1 + m3:m1 + m3 + m2]
 
-    def one(x, carry):
-        both = mul3((kron[0], kron[1]), (high_ref[0, x], low_ref[0, x])).astype(BF16)
-        for h in range(cols // SUB):
-            out_ref[:, x, h * SUB:(h + 1) * SUB, :] = both[:, h * depth:(h + 1) * depth].reshape(
-                channels, SUB, depth)
-        return carry
-
-    lax.fori_loop(0, out_ref.shape[1], one, 0)
+    out_ref[...] = field_ref[...]
     per = core_ref.shape[2]
 
     def two(a, carry):
@@ -780,12 +809,11 @@
     piece = (r2 // py, count // px, LANES)
     pack = (ri + r1, LANES)
     core = tucker_core.transpose(0, 2, 3, 4, 1)
-    high, low, core_sum, packed = pl.pallas_call(
+    field, core_sum, packed = pl.pallas_call(
         functools.partial(remote_kernel, px, py),
-        out_shape=(shape((tiles,) + real, BF16), shape((tiles,) + real, BF16),
-                   shape((px, py) + piece, F32), shape(pack, F32)),
+        out_shape=(shape(flow_field.shape, BF16), shape((px, py) + piece, F32), shape(pack, F32)),
         in_specs=[smem] + [anywhere] * 5 + [vmem] * 9,
-        out_specs=(anywhere, anywhere, vmem, vmem),
+        out_specs=(anywhere, vmem, vmem),
         scratch_shapes=[
             thin(steps, channels, group, cols, depth),
             thin(2, 2 * ri * SUB, channels * SUB),
@@ -797,14 +825,14 @@
             buf(*spectrum), buf(*spectrum), buf(2, *spectrum),
             buf(count * r3, LANES), buf(count, wide), buf(M1, ri * wide),
             buf(2, px, tiles, 2 * group, wide), buf(steps, py, *block),
-            thin(lines, 2 * LANES), thin(lines, 2 * LANES), thin(tiles + 1, *real), thin(tiles + 1, *real),
+            thin(2, channels * SUB, ro * SUB), thin(tiles + 1, *real), thin(tiles + 1, *real),
             buf(2, channels * SUB, ri * SUB),
             buf(count, LANES), buf(px, count // px, LANES), buf(py, *piece), buf(py, *piece),
             buf(px, py, *piece), buf(2, *pack), buf(px, *pack), buf(py, *pack),
             dma((steps,)), dma((3,)),
             dma((steps, 2)), dma((steps, 2)), dma((steps,)), dma((steps,)), dma((steps, px)), dma((steps, px)),
             dma((steps, px)), dma((steps, px)), dma((steps,)), dma((steps,)), dma((steps, 2)), dma((steps, 2)),
-            dma((tiles, 2)),
+            dma((tiles,)),
             dma((px,)), dma((px,)), dma((py,)), dma((py,)), dma((px,)), dma((px,)), dma((3,)), dma((3,)),
             dma((px,)), dma((px,)), dma((py,)), dma((py,)),
         ],
@@ -823,19 +851,17 @@
             shape((ro, channels), F32), shape((r1, M1), F32), shape((r2, M2), F32), shape((r3, M3), F32),
         ),
         in_specs=[
-            pl.BlockSpec((1, span) + real[1:], lambda i: (i * span // group, i % (group // span), 0, 0)),
-            pl.BlockSpec((1, span) + real[1:], lambda i: (i * span // group, i % (group // span), 0, 0)),
+            pl.BlockSpec((channels, span, cols, depth), lambda i: (0, i, 0, 0)),
             pl.BlockSpec((1,) + (py,) + piece, lambda i: (i, 0, 0, 0, 0)),
-            whole(*pack), whole(ro, channels),
+            whole(*pack),
         ],
         out_specs=(
             pl.BlockSpec((channels, span, cols, depth), lambda i: (0, i, 0, 0)),
             pl.BlockSpec((ri // px, r1, r2, r3, ro), lambda i: (i, 0, 0, 0, 0)),
             whole(ri, channels), whole(ro, channels), whole(r1, M1), whole(r2, M2), whole(r3, M3),
         ),
-        scratch_shapes=[thin(2, channels * SUB, ro * SUB)],
         compiler_params=pltpu.CompilerParams(vmem_limit_bytes=VMEM_LIMIT),
-    )(high, low, core_sum, packed, out_factor.T)
+    )(field, core_sum, packed)
     return (out, core_grad.transpose(0, 4, 1, 2, 3), in_grad.T, out_grad.T, first_grad.T, second_grad.T,
             third_grad.T)
 

time: 125 us -> 124 us (level)
    pallas_call x1, Pallas kernels: 14.7 us -> 10.8 us  [fast_shards(): pl.pallas_call(emit_kernel, grid=(px,), out_shape=(shape(flow_field.shape...]
    pallas_call x1, Pallas kernels: 110 us -> 113 us  [fast_shards(): pl.pallas_call(functools.partial(remote_kernel, px, py), out_shape=(shape...]
where the time goes in v2:
time: 124 us
  Pallas kernels  123 us (99%)
    pallas_call x1, Pallas kernels, fast_shards(): pl.pallas_call(functools.partial(remote_kernel, px, py), out_shape=(shape...  113 us
    pallas_call x1, Pallas kernels, fast_shards(): pl.pallas_call(emit_kernel, grid=(px,), out_shape=(shape(flow_field.shape...  10.8 us

profile of v2, /device:TPU:0, one launch (start us, length us, event | category | flops | bytes accessed | tf_op | source)
XLA Modules:
  0.0 124.1 jit_solution(18242286275659346285)
XLA Ops:
  0.6 112.6 %shard_map.198 = (bf16[64,16,32,128]{3,2,1,0:T(8,128)(2,1)}, f32[8,4,2,16,128]{4,3,2,1,0:T(8,128)}, f32[24,128]{1,0:T(8,128)}) custom-call(f32[8,32]{1,0:T(8,128)} %bitcast.15, bf16[64,16,32,128]{3,2,1,0:T(8,128)(2,1)} %flow_ref.1, bf16[64,16,32,128]{3,2,1,0:T(8,128)(2,1)} %cot_ref.1, bf16[4,2,256,256]{3,2,1,0:T(8,128)(2,1)} %constant.15.clone.tyf_ref, ...), custom_call_target="tpu_custom_call" | custom-call | tf_op jit(solution)/shard_map/pallas_call | solution.py:812
  113.3 10.8 %shard_map.199 = (bf16[64,16,32,128]{3,2,1,0:T(8,128)(2,1)}, f32[16,8,8,8,16]{4,3,2,1,0:T(8,128)}, f32[16,64]{1,0:T(8,128)}, f32[16,64]{1,0:T(8,128)}, f32[8,32]...) custom-call(bf16[64,16,32,128]{3,2,1,0:T(8,128)(2,1)} %get-tuple-element.17.field_ref, ...), custom_call_target="tpu_custom_call" | custom-call | tf_op jit(solution)/shard_map/pallas_call | solution.py:847

commit v3 on v2

--- a/solution.py
+++ b/solution.py
@@ -275,20 +275,26 @@
     wide = packs * LANES
 
     here.greet()
-    for t in range(steps):
+
+    def load(t):
         source = flow_ref if t < tiles else cot_ref
         pltpu.make_async_copy(
             source.at[:, pl.ds((t % tiles) * group, group)], tile.at[t], load_sem.at[t]).start()
+
+    load(0)
     tables = [pltpu.make_async_copy(tyf_ref.at[q], tyf, table_sem.at[0]),
               pltpu.make_async_copy(tyb_ref.at[q], tyb, table_sem.at[1]),
               pltpu.make_async_copy(core_ref, core, table_sem.at[2])]
-    for copy in tables[:2]:
-        copy.start()
+    tables[0].start()
+    load(1)
     for f, weight in enumerate((win_ref, wout_ref)):
         high, low = spread(weight[...], NN)
         kron[f, :ranks * SUB] = high
         kron[f, ranks * SUB:] = low
     totals[...] = jnp.zeros_like(totals)
+    for t in range(2, steps):
+        load(t)
+    tables[1].start()
     tables[0].wait()
 
     def mate_copies(t):
@@ -515,12 +521,6 @@
     rows_out(0)
     arrive(1)
     lax.fori_loop(0, ranks, unblend, 0)
-    rows_out(1)
-    tables[1].wait()
-    high, low = spread(wout_ref[...], NT)
-    krono[0] = high
-    krono[1] = low
-
     def tall_grads():
         thin = exact(first_ref[...], grads[...])
         return jnp.concatenate([thin[:, a * wide:(a + 1) * wide] for a in range(ranks)], axis=0)
@@ -557,6 +557,10 @@
         for s in range(r2):
             small = small + jnp.where((lane == k + m1 + m3) & (row == s), jnp.sum(sums[s]), 0.0)
         pack_sum[0, ranks:ranks + r1] = small
+
+    core_side()
+    rows_out(1)
+    tables[1].wait()
 
     def slot(t):
         return (t + 1) * (1 - t // tiles)
@@ -601,7 +605,7 @@
     def out_copy(g):
         return pltpu.make_async_copy(tile.at[tiles + g], out_ref.at[:, pl.ds(g * group, group)], out_sem.at[g])
 
-    def emit(g):
+    def emit(g, carry):
         def one(x, carry):
             both = mul3((krono[0], krono[1]), (real_h[g + 1, x], real_l[g + 1, x])).astype(BF16)
             for h in range(cols // SUB):
@@ -611,6 +615,7 @@
 
         lax.fori_loop(0, group, one, 0)
         out_copy(g).start()
+        return carry
 
     def back_body(i, carry):
         @pl.when(i < steps)
@@ -633,17 +638,15 @@
             place(t)
             outer(t)
 
-        @pl.when((i >= tiles + 1) & (i < tiles + 3))
-        def _():
-            emit(i - tiles - 1)
-
-        @pl.when(i == 2)
-        def _():
-            core_side()
-
-        @pl.when(i == 3)
+        @pl.when(i == 0)
         def _():
             small_side()
+
+        @pl.when(i == 1)
+        def _():
+            high, low = spread(wout_ref[...], NT)
+            krono[0] = high
+            krono[1] = low
 
         @pl.when(i == 5)
         def _():
@@ -689,7 +692,7 @@
     for step in range(1, px):
         pr_copy(step).start()
     pack_row[p] = pack_sum[0]
-    emit(tiles - 2)
+    lax.fori_loop(0, tiles // 2, emit, 0)
     bg_copy(1).wait_recv()
     bg_copy(2).wait_recv()
     core_out[...] = core_all[...]
@@ -702,7 +705,7 @@
     for step in range(1, py):
         pc_copy(step).start()
     pack_col[q] = total
-    emit(tiles - 1)
+    lax.fori_loop(tiles // 2, tiles, emit, 0)
 
     def drain(t, carry):
         for copy in mate_copies(t):
@@ -736,31 +739,50 @@
 
 
 def emit_kernel(field_ref, core_ref, pack_ref, out_ref, core_out, in_out, oo_out,
-                first_out, second_out, third_out):
+                first_out, second_out, third_out, tile, core, load_sem, store_sem, core_sem):
     ranks, channels = in_out.shape
     _, r1, r2, r3, _ = core_out.shape
     m1, m3 = first_out.shape[1], third_out.shape[1]
     m2 = second_out.shape[1]
-
-    @pl.when(pl.program_id(0) == 0)
-    def _():
-        in_out[...] = pack_ref[:ranks, :channels]
-        oo_out[...] = pack_ref[:ranks, channels:2 * channels]
-        first_out[...] = pack_ref[ranks:ranks + r1, :m1]
-        third_out[...] = pack_ref[ranks:ranks + r1, m1:m1 + m3]
-        second_out[...] = pack_ref[ranks:ranks + r1, m1 + m3:m1 + m3 + m2]
-
-    out_ref[...] = field_ref[...]
+    tiles, _, group = tile.shape[:3]
     per = core_ref.shape[2]
-
-    def two(a, carry):
+    share = ranks // tiles
+    pair = core_ref.shape[3] // r1
+
+    def load(g):
+        return pltpu.make_async_copy(field_ref.at[:, pl.ds(g * group, group)], tile.at[g], load_sem.at[g])
+
+    def store(g):
+        return pltpu.make_async_copy(tile.at[g], out_ref.at[:, pl.ds(g * group, group)], store_sem.at[g])
+
+    def lay(g):
+        part = pl.ds(g * share, share)
+        return pltpu.make_async_copy(core.at[part], core_out.at[part], core_sem.at[g])
+
+    for g in range(tiles):
+        load(g).start()
+
+    def one(a, carry):
         for s in range(r2):
-            rows = core_ref[0, s // per, s % per, pl.ds(pl.multiple_of(a * r1, r1), r1), :]
+            spot = pl.ds(pl.multiple_of(lax.rem(a, pair) * r1, r1), r1)
+            rows = core_ref[a // pair, s // per, s % per, spot, :]
             for r in range(r1):
-                core_out[a, r, s] = unfold(rows[r:r + 1], r3, ranks)[:, :ranks]
+                core[a, r, s] = unfold(rows[r:r + 1], r3, ranks)[:, :ranks]
         return carry
 
-    lax.fori_loop(0, core_out.shape[0], two, 0)
+    for g in range(tiles):
+        lax.fori_loop(g * share, (g + 1) * share, one, 0)
+        lay(g).start()
+        load(g).wait()
+        store(g).start()
+    in_out[...] = pack_ref[:ranks, :channels]
+    oo_out[...] = pack_ref[:ranks, channels:2 * channels]
+    first_out[...] = pack_ref[ranks:ranks + r1, :m1]
+    third_out[...] = pack_ref[ranks:ranks + r1, m1:m1 + m3]
+    second_out[...] = pack_ref[ranks:ranks + r1, m1 + m3:m1 + m3 + m2]
+    for g in range(tiles):
+        lay(g).wait()
+        store(g).wait()
 
 
 def fast_shards(px, py, flow_field, cotangent, tucker_core, in_factor, out_factor,
@@ -842,24 +864,18 @@
       out_factor.T, first_factor.T, third_factor.T, scale,
       jnp.asarray(tz_f), jnp.asarray(tx_f), jnp.asarray(tz_b), jnp.asarray(tx_b))
 
-    span = rows // px
-    whole = lambda *dims: pl.BlockSpec(dims, lambda i: (0,) * len(dims))
     out, core_grad, in_grad, out_grad, first_grad, second_grad, third_grad = pl.pallas_call(
-        emit_kernel, grid=(px,),
+        emit_kernel,
         out_shape=(
             shape(flow_field.shape, BF16), shape(core.shape, F32), shape((ri, channels), F32),
             shape((ro, channels), F32), shape((r1, M1), F32), shape((r2, M2), F32), shape((r3, M3), F32),
         ),
-        in_specs=[
-            pl.BlockSpec((channels, span, cols, depth), lambda i: (0, i, 0, 0)),
-            pl.BlockSpec((1,) + (py,) + piece, lambda i: (i, 0, 0, 0, 0)),
-            whole(*pack),
+        in_specs=[anywhere, vmem, vmem],
+        out_specs=(anywhere, anywhere) + (vmem,) * 5,
+        scratch_shapes=[
+            thin(tiles, channels, group, cols, depth), buf(*core.shape),
+            dma((tiles,)), dma((tiles,)), dma((tiles,)),
         ],
-        out_specs=(
-            pl.BlockSpec((channels, span, cols, depth), lambda i: (0, i, 0, 0)),
-            pl.BlockSpec((ri // px, r1, r2, r3, ro), lambda i: (i, 0, 0, 0, 0)),
-            whole(ri, channels), whole(ro, channels), whole(r1, M1), whole(r2, M2), whole(r3, M3),
-        ),
         compiler_params=pltpu.CompilerParams(vmem_limit_bytes=VMEM_LIMIT),
     )(field, core_sum, packed)
     return (out, core_grad.transpose(0, 4, 1, 2, 3), in_grad.T, out_grad.T, first_grad.T, second_grad.T,

time: 124 us -> 119 us (0.960)
  Pallas kernels: 123 us -> 118 us
    pallas_call x1, Pallas kernels: 113 us -> 109 us  [fast_shards(): pl.pallas_call(functools.partial(remote_kernel, px, py), out_shape=(shape...]
    pallas_call x1, Pallas kernels: 10.8 us -> 9.54 us  [fast_shards(): pl.pallas_call(emit_kernel, out_shape=(shape(flow_field.shape, BF16), sha...]
where the time goes in v3:
time: 119 us
  Pallas kernels  118 us (99%)
    pallas_call x1, Pallas kernels, fast_shards(): pl.pallas_call(functools.partial(remote_kernel, px, py), out_shape=(shape...  109 us
    pallas_call x1, Pallas kernels, fast_shards(): pl.pallas_call(emit_kernel, out_shape=(shape(flow_field.shape, BF16), sha...  9.54 us

profile of v3, /device:TPU:0, one launch (start us, length us, event | category | flops | bytes accessed | tf_op | source)
XLA Modules:
  0.0 118.7 jit_solution(5296461411214537028)
XLA Ops:
  0.6 108.6 %shard_map.198 = (bf16[64,16,32,128]{3,2,1,0:T(8,128)(2,1)}, f32[8,4,2,16,128]{4,3,2,1,0:T(8,128)}, f32[24,128]{1,0:T(8,128)}) custom-call(f32[8,32]{1,0:T(8,128)} %bitcast.15, bf16[64,16,32,128]{3,2,1,0:T(8,128)(2,1)} %flow_ref.1, bf16[64,16,32,128]{3,2,1,0:T(8,128)(2,1)} %cot_ref.1, bf16[4,2,256,256]{3,2,1,0:T(8,128)(2,1)} %constant.15.clone.tyf_ref, ...), custom_call_target="tpu_custom_call" | custom-call | tf_op jit(solution)/shard_map/pallas_call | solution.py:834
  109.2 9.5 %shard_map.199 = (bf16[64,16,32,128]{3,2,1,0:T(8,128)(2,1)}, f32[16,8,8,8,16]{4,3,2,1,0:T(8,128)}, f32[16,64]{1,0:T(8,128)}, f32[16,64]{1,0:T(8,128)}, f32[8,32]...) custom-call(bf16[64,16,32,128]{3,2,1,0:T(8,128)(2,1)} %get-tuple-element.17.field_ref, ...), custom_call_target="tpu_custom_call" | custom-call | tf_op jit(solution)/shard_map/pallas_call | solution.py:867
